TPU v7x, 32 devices: a whole 2x2x4 slice. The times are simulated.
32 devices in a mesh: occ: 16 (over z, y, x), aux: 2 (over core).
Axes of the slice: x: 2, y: 2, z: 4, core: 2. Of those that a mesh axis runs over, the one named last changes fastest.
Arguments:
- factors: bfloat16 [7680, 16, 768], P('aux', 'occ'), may hold values from -0.71875 to 0.71875
- occ_energy: float32 [16], replicated, may hold values from -3 to -0.3
- virt_energy: float32 [768], replicated, may hold values from 0.3 to 3
Outputs:
- gradient: float32 [7680, 16, 768], P('aux', 'occ')
All inputs are finite; a program needn't handle non-finite values.
Results may differ from a plain program's by a relative error of at most 0.0027.
Values may be sent and summed in bfloat16 or wider, within the bound.
No kernel may reach another device: no remote copies, remote signals or barrier semaphores. Data moves between devices by JAX's collectives and lax.ppermute only.
A program may use at most 64 MiB of HBM per device.

v0:
```python
import jax
import jax.numpy as jnp
from jax import lax
from jax.sharding import PartitionSpec as P


def passed_along(value, axis, steps):
    count = lax.axis_size(axis)
    pairs = [(source, (source + steps) % count) for source in range(count)]
    return lax.ppermute(value, axis, pairs)


def pair_tilde(left, right, e_left, e_right, virt_energy):
    partial_sum = lax.dot_general(
        left, right, (((0,), (0,)), ((), ())), preferred_element_type=jnp.float32
    )
    width = virt_energy.shape[0]
    count = e_left.shape[0]
    whole = lax.psum(partial_sum, "aux")
    denom = (
        virt_energy[None, :, None, None]
        + virt_energy[None, None, None, :]
        - e_left[:, None, None, None]
        - e_right[None, None, :, None]
    )
    amplitude = whole.reshape(count, width, count, width) / denom
    tilde = (2.0 * amplitude - amplitude.transpose(0, 3, 2, 1)).astype(jnp.bfloat16)
    return tilde.reshape(count * width, count * width)


def local(factors, occ_energy, virt_energy):
    rows, count, width = factors.shape
    n_blocks = lax.axis_size("occ")
    offset = n_blocks // 4
    index = lax.axis_index("occ")
    own_rows = factors.reshape(rows, count * width)
    ahead = passed_along(factors, "occ", -offset)
    ahead_rows = ahead.reshape(rows, count * width)
    e_own = lax.dynamic_slice_in_dim(occ_energy, index * count, count)
    e_ahead = lax.dynamic_slice_in_dim(occ_energy, (index + offset) % n_blocks * count, count)
    tilde = pair_tilde(own_rows, ahead_rows, e_own, e_ahead, virt_energy)
    own_grad = lax.dot_general(
        ahead_rows, tilde, (((1,), (1,)), ((), ())), preferred_element_type=jnp.float32
    )
    behind = passed_along(factors, "occ", offset)
    behind_rows = behind.reshape(rows, count * width)
    e_behind = lax.dynamic_slice_in_dim(occ_energy, (index - offset) % n_blocks * count, count)
    tilde_back = pair_tilde(behind_rows, own_rows, e_behind, e_own, virt_energy)
    received = jnp.dot(behind_rows, tilde_back, preferred_element_type=jnp.float32)
    return (own_grad + received).reshape(rows, count, width)


def solution(mesh):
    in_specs = (P("aux", "occ", None), P(), P())
    out_specs = P("aux", "occ", None)
    return jax.shard_map(local, mesh=mesh, in_specs=in_specs, out_specs=out_specs, check_vma=False)
```

profile of v0, /device:TPU:0, one launch (start us, length us, event | category | flops | bytes accessed | tf_op | source)
XLA Modules:
  0.0 382.2 jit_solution(16881376789325307993)
XLA Ops:
  6.5 0.0 all-reduce.3.cloned.1.call-start
  6.5 0.0 copy-start.3
  6.5 3.1 collective-permute-start.1
  9.6 2.0 collective-permute-start
  11.6 128.3 %collective-permute-done.1 = bf16[3840,1,768]{2,0,1:T(8,128)(2,1)S(1)} collective-permute-done((bf16[3840,1,768]{2,0,1:T(8,128)(2,1)}, bf16[3840,1,768]{2,0,1:T(8,128)(2,1)S(1)}, u32[]{:S(2)}, u32[]{:S(2)}) %collective-permute-start.1) | collective-permute-done | bytes 5898272 | tf_op jit(solution)/shard_map/ppermute | solution.py:10
  139.9 0.0 copy-start.4
  139.9 11.1 %fusion.2 = f32[768,768]{1,0:T(8,128)} fusion(bf16[3840,1,768]{2,0,1:T(8,128)(2,1)S(1)} %collective-permute-done.1, bf16[3840,1,768]{2,0,1:T(8,128)(2,1)} %param.3), kind=kOutput, calls=%fused_computation.3 | convolution fusion | flops 4529848320 | bytes 14155776 | tf_op jit(solution)/shard_map/dot_general | solution.py:14
  150.9 0.0 copy-done.4
  150.9 113.8 %collective-permute-done = bf16[3840,1,768]{2,0,1:T(8,128)(2,1)S(1)} collective-permute-done((bf16[3840,1,768]{2,0,1:T(8,128)(2,1)}, bf16[3840,1,768]{2,0,1:T(8,128)(2,1)S(1)}, u32[]{:S(2)}, u32[]{:S(2)}) %collective-permute-start) | collective-permute-done | bytes 5898272 | tf_op jit(solution)/shard_map/ppermute | solution.py:10
  264.7 0.0 copy-start.5
  264.7 2.5 copy-done.5
  267.3 0.0 copy-done.3
  267.3 6.3 %fusion.5 = f32[768,768]{1,0:T(8,128)} fusion(bf16[3840,1,768]{2,0,1:T(8,128)(2,1)S(1)} %collective-permute-done, bf16[3840,1,768]{2,0,1:T(8,128)(2,1)S(1)} %copy-done.3), kind=kOutput, calls=%fused_computation.6 | convolution fusion | flops 4529848320 | bytes 14155776 | tf_op jit(solution)/shard_map/dot_general | solution.py:14
  273.6 0.0 copy-start.2
  273.6 0.0 copy-start.1
  273.6 0.0 all-reduce.3.cloned.1.call-update
  273.7 0.6 copy-done.2
  274.3 0.7 fusion.23
  274.9 38.9 %all-reduce.3.cloned.1.call-done = (f32[768,768]{1,0:T(8,128)}, f32[768,768]{1,0:T(8,128)}) async-done(((f32[768,768]{1,0:T(8,128)}, f32[768,768]{1,0:T(8,128)}), (f32[768,768]{1,0:T(8,128)}, f32[768,768]{1,0:T(8,128)})) %all-reduce.3.cloned.1.call-update) | async-done | bytes 4718608 | tf_op jit(solution)/shard_map/psum | solution.py:19
  313.8 0.0 copy-done.1
  313.8 6.5 %fusion.10 = (f32[768,768]{1,0:T(8,128)S(1)}, f32[768,768]{1,0:T(8,128)}) fusion(f32[768,768]{1,0:T(8,128)} %get-tuple-element.6, f32[]{:T(128)} %bitcast.3, f32[]{:T(128)} %bitcast.2, f32[768]{0:T(1024)S(1)} %copy-done.1, f32[768,768]{1,0:T(8,128)} %get-tuple-element.5, f32[]{:T(128)} %bitcast.9), kind=kLoop, calls=%fused_computation.13 | loop fusion | flops 4128768 | bytes 9440268 | tf_op jit(solution)/shard_map/div | solution.py:26
  320.3 3.1 copy.5
  323.4 2.0 copy.4
  325.4 0.0 copy-start
  325.4 13.5 %fusion = f32[768,3840]{1,0:T(8,128)} fusion(bf16[3840,1,768]{2,0,1:T(8,128)(2,1)} %copy-done.4, f32[768,768]{1,0:T(8,128)} %get-tuple-element.8, f32[768,768]{0,1:T(8,128)} %copy.5), kind=kOutput, calls=%fused_computation.1 | convolution fusion | flops 4531617792 | bytes 22413312 | tf_op jit(solution)/shard_map/dot_general | solution.py:49
  338.9 0.0 copy-done
  338.9 12.0 %add_bitcast_fusion = f32[3840,1,768]{0,2,1:T(8,128)} fusion(f32[768,3840]{1,0:T(8,128)} %fusion, bf16[3840,1,768]{2,0,1:T(8,128)(2,1)} %copy-done.5, f32[768,768]{1,0:T(8,128)S(1)} %get-tuple-element.7, f32[768,768]{0,1:T(8,128)S(1)} %copy-done), kind=kOutput, calls=%fused_computation | convolution fusion | flops 4534566912 | bytes 34209792 | tf_op jit(solution)/shard_map/dot_general | solution.py:42
  350.9 24.5 %copy.6 = f32[3840,1,768]{2,1,0:T(1,128)} copy(f32[3840,1,768]{0,2,1:T(8,128)} %add_bitcast_fusion) | data formatting | bytes 23592960 | tf_op jit(solution)/shard_map/reshape | solution.py:50
Async XLA Ops:
  6.5 307.2 %all-reduce.3.cloned.1.call-start = ((), (), s32[]{:S(2)}) async-start(), calls=%async_computation | async-start | bytes 9437184 | tf_op jit(solution)/shard_map/psum | solution.py:19
  6.5 260.8 %copy-start.3 = (bf16[3840,1,768]{2,0,1:T(8,128)(2,1)S(1)}, bf16[3840,1,768]{2,0,1:T(8,128)(2,1)}, u32[]{:S(2)}) copy-start(bf16[3840,1,768]{2,0,1:T(8,128)(2,1)} %param.3) | copy-start | bytes 17694724
  6.5 133.3 %collective-permute-start.1 = (bf16[3840,1,768]{2,0,1:T(8,128)(2,1)}, bf16[3840,1,768]{2,0,1:T(8,128)(2,1)S(1)}, u32[]{:S(2)}, u32[]{:S(2)}) collective-permute-start(bf16[3840,1,768]{2,0,1:T(8,128)(2,1)} %param.3), channel_id=1, source_target_pairs={{0,8},{2,10},{4,12},{6,14},{8,16},{10,18},{12,20},{14,22},{16,24},... | collective-permute-start | bytes 17694728 | tf_op jit(solution)/shard_map/ppermute | solution.py:10
  9.6 255.2 %collective-permute-start = (bf16[3840,1,768]{2,0,1:T(8,128)(2,1)}, bf16[3840,1,768]{2,0,1:T(8,128)(2,1)S(1)}, u32[]{:S(2)}, u32[]{:S(2)}) collective-permute-start(bf16[3840,1,768]{2,0,1:T(8,128)(2,1)} %param.3), channel_id=1, source_target_pairs={{0,24},{2,26},{4,28},{6,30},{8,0},{10,2},{12,4},{14,6},{16,8},{18,... | collective-permute-start | bytes 17694728 | tf_op jit(solution)/shard_map/ppermute | solution.py:10
  139.9 11.1 %copy-start.4 = (bf16[3840,1,768]{2,0,1:T(8,128)(2,1)}, bf16[3840,1,768]{2,0,1:T(8,128)(2,1)S(1)}, u32[]{:S(2)}) copy-start(bf16[3840,1,768]{2,0,1:T(8,128)(2,1)S(1)} %collective-permute-done.1) | copy-start | bytes 17694724
  264.7 2.5 copy-start.5
  273.6 0.7 copy-start.2
  273.6 40.2 %copy-start.1 = (f32[768]{0:T(1024)S(1)}, f32[768]{0:T(1024)}, u32[]{:S(2)}) copy-start(f32[768]{0:T(1024)} %param.5) | copy-start | bytes 9220
  325.4 13.5 %copy-start = (f32[768,768]{0,1:T(8,128)S(1)}, f32[768,768]{0,1:T(8,128)}, u32[]{:S(2)}) copy-start(f32[768,768]{0,1:T(8,128)} %copy.4) | copy-start | bytes 7077892
Sparse Core Ops, SparseCore 0:
  273.8 39.9 all-reduce.2
where the time goes:
time: 383 us; the launch traced here: 382 us
  waiting for transfers between devices  281 us (73%)
  matrix products  42.9 us (11%)
  local copies, waits for them, and re-layouts  33.3 us (9%)
  between operations  13.4 us (3%)
  other arithmetic  6.52 us (2%)
  starting transfers between devices  5.08 us (1%)
    ppermute x2, waiting for transfers between devices, passed_along(): return lax.ppermute(value, axis, pairs)  242 us
    psum x1, waiting for transfers between devices, pair_tilde(): whole = lax.psum(partial_sum, 'aux')  38.9 us
    reshape x1, local copies, waits for them, and re-layouts, local(): return (own_grad + received).reshape(rows, count, width)  24.5 us
    dot_general x2, matrix products, pair_tilde(): lax.dot_general(left, right, (((0,), (0,)), ((), ())), preferred_element_...  17.4 us
    dot_general x1, matrix products, local(): jnp.dot(behind_rows, tilde_back, preferred_element_type=jnp.float32)  13.5 us
    dot_general x1, matrix products, local(): lax.dot_general(ahead_rows, tilde, (((1,), (1,)), ((), ())), preferred_el...  12 us
  transfers between devices with their start and end apart: 3, of which 3 were waited for; matrix products, arithmetic and copies ran while one was open for 3% of the time, Pallas kernels for 0%

commit v1 on v0

v1 whole, which is shorter than its diff:
```python
import functools
import math

import jax
import jax.numpy as jnp
from jax import lax
from jax.experimental import pallas as pl
from jax.experimental.pallas import tpu as pltpu
from jax.sharding import PartitionSpec as P


LANES = 128
F32 = jnp.float32
BF16 = jnp.bfloat16
ROWS_IN = (((0,), (0,)), ((), ()))


def largest_block(rows, most):
    return max(size for size in range(16, most + 1, 16) if rows % size == 0)


def swapped(value):
    return lax.ppermute(value, "aux", [(0, 1), (1, 0)])


def aux_terms(value):
    if lax.axis_size("aux") == 2:
        return [value, swapped(value)]
    return [lax.psum(value, "aux")]


def gram(left, right):
    return lax.dot_general(left, right, ROWS_IN, preferred_element_type=F32)


def on_chip(value):
    return pltpu.with_memory_space_constraint(value, pltpu.VMEM)


def fill_tilde(tilde, amp, sums, pairs, across, e_left, e_right):
    width = tilde.shape[0]
    for at in range(0, width, LANES):
        here = pl.ds(at, LANES)
        whole = sums[0][here, :]
        for other in sums[1:]:
            whole = whole + other[here, :]
        for left, right in pairs:
            whole = whole + gram(left[:, at : at + LANES], right[...])
        down = jnp.transpose(jnp.broadcast_to(across[:, at : at + LANES], (LANES, LANES)))
        amp[here, :] = whole / (down[:, :1] + across - e_left - e_right)
    for at in range(0, width, LANES):
        here = pl.ds(at, LANES)
        tilde[here, :] = (2.0 * amp[here, :] - jnp.transpose(amp[:, at : at + LANES])).astype(BF16)


def gram_kernel(block, offset, has_start, *refs):
    start, left, right, out = refs if has_start else (None, *refs)
    out[...] = start[...] if has_start else jnp.zeros_like(out)

    @pl.loop(0, left.shape[0] // block)
    def _(step):
        rows = left[pl.ds(pl.multiple_of(step * block, block), block), :]
        others = right[pl.ds(pl.multiple_of(offset + step * block, math.gcd(offset, block)), block), :]
        out[...] += gram(rows, others)


def gram_stage(left, right, offset=0, start=None):
    width = right.shape[1]
    vmem = pl.BlockSpec(memory_space=pltpu.VMEM)
    operands = [value for value in (start, left, right) if value is not None]
    return pl.pallas_call(
        functools.partial(gram_kernel, largest_block(left.shape[0], 640), offset, start is not None),
        in_specs=[vmem] * len(operands),
        out_specs=vmem,
        out_shape=pltpu.VMEM((width, width), F32),
        compiler_params=pltpu.CompilerParams(vmem_limit_bytes=10 << 20),
        cost_estimate=pl.CostEstimate(flops=2 * left.size * width, bytes_accessed=0, transcendentals=0),
        name="gram_stage",
    )(*[on_chip(value) for value in operands])


def near_kernel(block, n_sums, energy, virt_row, *refs):
    sums, (behind, ahead, out, amp, *tildes) = refs[: 2 * n_sums], refs[2 * n_sums :]
    across = virt_row[...]
    for item, tilde in enumerate(tildes):
        terms = sums[item * n_sums : (item + 1) * n_sums]
        fill_tilde(tilde, amp, terms, [], across, energy[2 * item], energy[2 * item + 1])

    @pl.loop(0, out.shape[0] // block)
    def _(step):
        here = pl.ds(pl.multiple_of(step * block, block), block)
        first = jnp.dot(behind[here, :], tildes[0][...], preferred_element_type=F32)
        out[here, :] = first + jnp.dot(ahead[here, :], tildes[1][...], preferred_element_type=F32)


def near_stage(energy, virt_row, sums, behind, ahead, block):
    rows, width = behind.shape
    vmem = pl.BlockSpec(memory_space=pltpu.VMEM)
    operands = [virt_row, *sums, behind, ahead]
    return pl.pallas_call(
        functools.partial(near_kernel, block, len(sums) // 2),
        in_specs=[pl.BlockSpec(memory_space=pltpu.SMEM)] + [vmem] * len(operands),
        out_specs=vmem,
        out_shape=pltpu.VMEM((rows, width), F32),
        scratch_shapes=[pltpu.VMEM((width, width), F32)] + [pltpu.VMEM((width, width), BF16)] * 2,
        compiler_params=pltpu.CompilerParams(vmem_limit_bytes=16 << 20),
        cost_estimate=pl.CostEstimate(flops=4 * rows * width * width, bytes_accessed=0, transcendentals=0),
        name="near_stage",
    )(energy, *[on_chip(value) for value in operands])


def far_kernel(block, n_sums, n_pairs, heights, energy, virt_row, *refs):
    refs = list(refs)
    sums = [refs.pop(0) for _ in range(n_sums)]
    pairs = [(refs.pop(0), refs.pop(0)) for _ in range(n_pairs)]
    parts = [refs.pop(0) for _ in heights]
    base, out, amp, tilde, out_buf, out_sem = refs
    width = tilde.shape[0]
    strips = width // LANES
    fill_tilde(tilde, amp, sums, pairs, virt_row[...], energy[0], energy[1])

    jobs, first = [], 0
    for part, height in zip(parts, heights):
        for at in range(0, height, block):
            jobs.append((part, at, first + at, min(block, height - at)))
        first += height

    def copy(job):
        _, _, row, tall = jobs[job]
        rows = pl.ds(0, tall * strips)
        return pltpu.make_async_copy(
            out_buf.at[job % 2, rows, :], out.at[pl.ds(row * strips, tall * strips), :], out_sem.at[job % 2]
        )

    for job, (part, at, row, tall) in enumerate(jobs):
        term = jnp.dot(part[pl.ds(at, tall), :], tilde[...], preferred_element_type=F32)
        result = base[pl.ds(row, tall), :] + term
        if job >= 2:
            copy(job - 2).wait()
        for strip in range(strips):
            out_buf[job % 2, pl.ds(strip, tall, strips), :] = result[:, strip * LANES : (strip + 1) * LANES]
        copy(job).start()
    for job in range(max(0, len(jobs) - 2), len(jobs)):
        copy(job).wait()


def far_stage(energy, virt_row, sums, pairs, parts, base, block):
    rows, width = base.shape
    strips = width // LANES
    vmem = pl.BlockSpec(memory_space=pltpu.VMEM)
    operands = [virt_row, *sums, *[value for pair in pairs for value in pair], *parts, base]
    heights = tuple(part.shape[0] for part in parts)
    return pl.pallas_call(
        functools.partial(far_kernel, block, len(sums), len(pairs), heights),
        in_specs=[pl.BlockSpec(memory_space=pltpu.SMEM)] + [vmem] * len(operands),
        out_specs=pl.BlockSpec(memory_space=pl.ANY),
        out_shape=jax.ShapeDtypeStruct((rows * strips, LANES), F32),
        scratch_shapes=[
            pltpu.VMEM((width, width), F32),
            pltpu.VMEM((width, width), BF16),
            pltpu.VMEM((2, block * strips, LANES), F32),
            pltpu.SemaphoreType.DMA((2,)),
        ],
        compiler_params=pltpu.CompilerParams(vmem_limit_bytes=20 << 20),
        cost_estimate=pl.CostEstimate(
            flops=2 * rows * width * width, bytes_accessed=4 * rows * width, transcendentals=0
        ),
        name="far_stage",
    )(energy, *[on_chip(value) for value in operands])


def plain(factors, occ_energy, virt_energy):
    rows, count, width = factors.shape
    n_blocks = lax.axis_size("occ")
    offset = n_blocks // 4
    index = lax.axis_index("occ")
    total = jnp.zeros((rows, count, width), F32)
    own_e = lax.dynamic_slice_in_dim(occ_energy, index * count, count)
    for steps, first in ((-offset, True), (offset, False)):
        ring = [(source, (source + steps) % n_blocks) for source in range(n_blocks)]
        other = lax.ppermute(factors, "occ", ring)
        other_e = lax.dynamic_slice_in_dim(occ_energy, (index - steps) % n_blocks * count, count)
        whole = sum(aux_terms(jnp.einsum("pja,pib->jaib", other, factors, preferred_element_type=F32)))
        e_left, e_right = (own_e[None, None, :, None], other_e[:, None, None, None])
        if not first:
            e_left, e_right = e_right, e_left
        amplitude = whole / (virt_energy[None, :, None, None] + virt_energy - e_left - e_right)
        tilde = (2.0 * amplitude - amplitude.transpose(0, 3, 2, 1)).astype(BF16)
        total = total + jnp.einsum("pja,jaib->pib", other, tilde, preferred_element_type=F32)
    return total


def far_cuts(rows, unit):
    steps = rows // unit
    if lax.axis_size("aux") != 2 or steps < 4:
        return [0, rows], 0
    return [0, (steps * 2 // 5) * unit, (steps * 4 // 5) * unit, (steps - 2) * unit, (steps - 1) * unit, rows], 2


def local(factors, occ_energy, virt_energy):
    rows, count, width = factors.shape
    n_blocks = lax.axis_size("occ")
    if count != 1 or width % LANES or rows % 16:
        return plain(factors, occ_energy, virt_energy)
    offset = n_blocks // 4
    index = lax.axis_index("occ")
    cuts, n_late = far_cuts(rows, largest_block(rows, 256))

    up = [(s, s + offset) for s in range(n_blocks - offset)]
    down = [(s + offset, s) for s in range(n_blocks - offset)]
    ends = [(s, s + n_blocks - offset) for s in range(offset)]
    ends = ends + [(t, s) for s, t in ends]

    own = factors.reshape(rows, width)
    pieces = [own[a:b] for a, b in zip(cuts[:-1], cuts[1:])]
    behind = lax.ppermute(own, "occ", up)
    ahead = lax.ppermute(own, "occ", down)
    *pieces, behind, ahead = lax.optimization_barrier((*pieces, behind, ahead))
    far = []
    for piece in pieces:
        far.append(lax.ppermute(piece, "occ", ends))

    e_own = occ_energy[index]
    e_ahead = occ_energy[(index + offset) % n_blocks]
    e_behind = occ_energy[(index - offset) % n_blocks]
    virt_row = virt_energy.reshape(1, width)

    last = index >= n_blocks - offset
    energy = jnp.stack([e_behind, e_own, e_own, e_ahead])
    far_energy = jnp.stack([jnp.where(last, e_own, e_behind), jnp.where(last, e_ahead, e_own)])
    others = [swapped(piece) for piece in pieces[len(pieces) - n_late :]]
    energy, far_energy, *others = lax.optimization_barrier((energy, far_energy, *others))
    grams = [gram_stage(behind, own), gram_stage(ahead, own)]
    sums = aux_terms(grams[0]) + aux_terms(grams[1])
    base = near_stage(energy, virt_row, sums, behind, ahead, largest_block(rows, 480))

    far[0], base = lax.optimization_barrier((far[0], base))
    early = None
    for part, at in list(zip(far, cuts))[: len(far) - n_late]:
        if early is not None:
            part, early = lax.optimization_barrier((part, early))
        early = gram_stage(part, own, at, early)
    sums = aux_terms(early)
    pairs = []
    for part, piece, other in zip(far[len(far) - n_late :], pieces[len(far) - n_late :], others):
        pairs += [(part, piece), (swapped(part), other)]
    out = far_stage(far_energy, virt_row, sums, pairs, far, base, largest_block(rows, 960))
    return out.reshape(rows, count, width)


def solution(mesh):
    in_specs = (P("aux", "occ", None), P(), P())
    out_specs = P("aux", "occ", None)

    return jax.shard_map(local, mesh=mesh, in_specs=in_specs, out_specs=out_specs, check_vma=False)
```

time: 383 us -> 308 us (0.80)
  waiting for transfers between devices: 281 us -> 209 us
  Pallas kernels: 0 us -> 54.1 us
  matrix products: 42.9 us -> 0 us
  starting transfers between devices: 5.08 us -> 26.3 us
  local copies, waits for them, and re-layouts: 33.3 us -> 13.3 us
  between operations: 13.4 us -> 2.94 us
  other arithmetic: 6.52 us -> 2.1 us
    pallas_call x0 -> x7, Pallas kernels: none -> 54.1 us  [the longest x5 25.9 us: gram_stage(): pl.pallas_call(functools.partial(gram_kernel, largest_block(left.shape[0]...]
    dot_general x4 -> x0, matrix products: 42.9 us -> none  [the longest x2 17.4 us: pair_tilde(): lax.dot_general(left, right, (((0,), (0,)), ((), ())), preferred_element_...]
    psum x1 -> x0, waiting for transfers between devices: 38.9 us -> none  [pair_tilde(): whole = lax.psum(partial_sum, 'aux')]
    ppermute x2 -> x14, waiting for transfers between devices: 242 us -> 209 us  [the longest x1 118 us: local(): behind = lax.ppermute(own, 'occ', up)]
    reshape x1, local copies, waits for them, and re-layouts: 24.5 us -> 0.01 us  [local(): virt_row = virt_energy.reshape(1, width)]
    ppermute x2 -> x14, starting transfers between devices: 5.08 us -> 26.3 us  [the longest x5 18.9 us: local(): far.append(lax.ppermute(piece, 'occ', ends))]
    slice x0 -> x2, local copies, waits for them, and re-layouts: none -> 7.3 us  [local(): pieces = [own[a:b] for a, b in zip(cuts[:-1], cuts[1:])]]
    div x1 -> x0, other arithmetic: 6.52 us -> none  [pair_tilde(): amplitude = whole.reshape(count, width, count, width) / denom]
  transfers between devices with their start and end apart: 3 -> 14, of which waited for: 3 -> 9; matrix products, arithmetic and copies ran while one was open for 3% -> 3% of each run, Pallas kernels for 0% -> 11%
where the time goes in v1:
time: 308 us
  waiting for transfers between devices  209 us (68%)
  Pallas kernels  54.1 us (18%)
  starting transfers between devices  26.3 us (9%)
  local copies, waits for them, and re-layouts  13.3 us (4%)
    ppermute x1, waiting for transfers between devices, local(): behind = lax.ppermute(own, 'occ', up)  118 us
    ppermute x5, waiting for transfers between devices, local(): far.append(lax.ppermute(piece, 'occ', ends))  83.3 us
    pallas_call x5, Pallas kernels, gram_stage(): pl.pallas_call(functools.partial(gram_kernel, largest_block(left.shape[0]...  25.9 us
    ppermute x5, starting transfers between devices, local(): far.append(lax.ppermute(piece, 'occ', ends))  18.9 us
    pallas_call x1, Pallas kernels, near_stage(): pl.pallas_call(functools.partial(near_kernel, block, len(sums) // 2), in_...  16.1 us
    pallas_call x1, Pallas kernels, far_stage(): pl.pallas_call(functools.partial(far_kernel, block, len(sums), len(pairs)...  12.1 us
    slice x2, local copies, waits for them, and re-layouts, local(): pieces = [own[a:b] for a, b in zip(cuts[:-1], cuts[1:])]  7.3 us
  transfers between devices with their start and end apart: 14, of which 9 were waited for; matrix products, arithmetic and copies ran while one was open for 3% of the time, Pallas kernels for 11%

profile of v1, /device:TPU:0, one launch (start us, length us, event | category | flops | bytes accessed | tf_op | source)
XLA Modules:
  0.0 307.6 jit_solution(17140732555781266536)
XLA Ops:
  0.0 5.3 %collective-permute-start = (bf16[3840,768]{1,0:T(8,128)(2,1)}, bf16[3840,768]{1,0:T(8,128)(2,1)S(1)}, u32[]{:S(2)}, u32[]{:S(2)}) collective-permute-start(bf16[3840,768]{1,0:T(8,128)(2,1)} %bitcast.17), channel_id=1, source_target_pairs={{0,8},{2,10},{4,12},{6,14},{8,16},{10,18},{12,20},{14,22},{16,24},... | collective-permute-start | bytes 17694728 | tf_op jit(solution)/shard_map/ppermute | solution.py:216
  5.3 1.3 collective-permute-start.1
  6.6 0.0 slice-start
  6.6 2.3 slice_bitcast_fusion.2
  8.9 5.0 %slice_bitcast_fusion = (bf16[1536,768]{1,0:T(8,128)(2,1)}, bf16[1536,768]{1,0:T(8,128)(2,1)}) fusion(bf16[3840,1,768]{2,0,1:T(8,128)(2,1)} %param.3), kind=kLoop, calls=%fused_computation | loop fusion | bytes 9437184 | tf_op jit(solution)/shard_map/slice | solution.py:215
  13.9 117.6 %collective-permute-done.refs_0_.refs_4_ = bf16[3840,768]{1,0:T(8,128)(2,1)S(1)} collective-permute-done((bf16[3840,768]{1,0:T(8,128)(2,1)}, bf16[3840,768]{1,0:T(8,128)(2,1)S(1)}, u32[]{:S(2)}, u32[]{:S(2)}) %collective-permute-start) | collective-permute-done | bytes 5898272 | tf_op jit(solution)/shard_map/ppermute | solution.py:216
  131.6 4.4 %collective-permute-done.1.refs_0_.refs_5_ = bf16[3840,768]{1,0:T(8,128)(2,1)S(1)} collective-permute-done((bf16[3840,768]{1,0:T(8,128)(2,1)}, bf16[3840,768]{1,0:T(8,128)(2,1)S(1)}, u32[]{:S(2)}, u32[]{:S(2)}) %collective-permute-start.1) | collective-permute-done | bytes 5898272 | tf_op jit(solution)/shard_map/ppermute | solution.py:217
  136.0 0.0 slice-done
  136.0 0.0 slice-done.1
  136.0 8.4 %gram_stage.5.refs_0_ = f32[768,768]{1,0:T(8,128)} custom-call(bf16[3840,768]{1,0:T(8,128)(2,1)S(1)} %collective-permute-done.refs_0_.refs_4_, bf16[3840,768]{1,0:T(8,128)(2,1)S(1)} %bitcast.21), custom_call_target="tpu_custom_call" | custom-call | flops 4529848320 | tf_op jit(solution)/shard_map/gram_stage/pallas_call | solution.py:71
  144.4 0.0 collective-permute-start.7
  144.4 0.0 slice-start.2
  144.4 8.4 %gram_stage.6.refs_2_ = f32[768,768]{1,0:T(8,128)} custom-call(bf16[3840,768]{1,0:T(8,128)(2,1)S(1)} %collective-permute-done.1.refs_0_.refs_5_, bf16[3840,768]{1,0:T(8,128)(2,1)S(1)} %bitcast.22), custom_call_target="tpu_custom_call" | custom-call | flops 4529848320 | tf_op jit(solution)/shard_map/gram_stage/pallas_call | solution.py:71
  152.9 0.5 collective-permute-start.8
  153.3 3.2 %collective-permute-start.6 = (bf16[1536,768]{1,0:T(8,128)(2,1)}, bf16[1536,768]{1,0:T(8,128)(2,1)}, u32[]{:S(2)}, u32[]{:S(2)}) collective-permute-start(bf16[1536,768]{1,0:T(8,128)(2,1)} %get-tuple-element.27), channel_id=1, source_target_pairs={{0,24},{2,26},{4,28},{6,30},{24,0},{26,2},{28,4},{30,6},{1,25},{3,... | collective-permute-start | bytes 7077896 | tf_op jit(solution)/shard_map/ppermute | solution.py:221
  156.5 4.4 %collective-permute-start.5 = (bf16[1536,768]{1,0:T(8,128)(2,1)}, bf16[1536,768]{1,0:T(8,128)(2,1)}, u32[]{:S(2)}, u32[]{:S(2)}) collective-permute-start(bf16[1536,768]{1,0:T(8,128)(2,1)} %get-tuple-element.26), channel_id=1, source_target_pairs={{0,24},{2,26},{4,28},{6,30},{24,0},{26,2},{28,4},{30,6},{1,25},{3,... | collective-permute-start | bytes 7077896 | tf_op jit(solution)/shard_map/ppermute | solution.py:221
  161.0 0.1 collective-permute-start.2
  161.1 1.7 collective-permute-done.2.refs_5_
  162.8 0.1 collective-permute-start.3
  162.9 0.7 fusion
  166.2 2.0 pad_maximum_fusion.energy
  168.2 0.1 pad_maximum_fusion.1.energy
  168.3 0.0 collective-permute-done.3.refs_9_
  168.3 3.5 %collective-permute-start.4 = (bf16[256,768]{1,0:T(8,128)(2,1)}, bf16[256,768]{1,0:T(8,128)(2,1)S(1)}, u32[]{:S(2)}, u32[]{:S(2)}) collective-permute-start(bf16[256,768]{1,0:T(8,128)(2,1)} %get-tuple-element.25), channel_id=1, source_target_pairs={{0,24},{2,26},{4,28},{6,30},{24,0},{26,2},{28,4},{30,6},{1,25},{3,... | collective-permute-start | bytes 1179656 | tf_op jit(solution)/shard_map/ppermute | solution.py:221
  171.8 0.0 collective-permute-done.7.refs_1_
  171.8 0.0 collective-permute-done.8.refs_3_
  171.8 0.0 copy-start.1
  171.8 2.7 copy-done.1
  174.5 2.7 copy-done.3
  177.1 16.1 %near_stage.1.refs_15_ = f32[3840,768]{1,0:T(8,128)S(1)} custom-call(f32[4]{0:T(128)S(1)} %pad_maximum_fusion.energy, f32[1,768]{1,0:T(1,128)S(1)} %reshape.15.virt_row, f32[768,768]{1,0:T(8,128)} %gram_stage.5.refs_0_, f32[768,768]{1,0:T(8,128)} %collective-permute-done.7.refs_1_, f32[768,768]{1,0:T(8,128)} %gram_stage.6.refs_2_, ...), custom_call_target="tpu_custom_call" | custom-call | flops 9059696640 | tf_op jit(solution)/shard_map/near_stage/pallas_call | solution.py:100
  193.3 18.2 %collective-permute-done.6.refs_0_.refs_10_ = bf16[1536,768]{1,0:T(8,128)(2,1)} collective-permute-done((bf16[1536,768]{1,0:T(8,128)(2,1)}, bf16[1536,768]{1,0:T(8,128)(2,1)}, u32[]{:S(2)}, u32[]{:S(2)}) %collective-permute-start.6) | collective-permute-done | bytes 2359328 | tf_op jit(solution)/shard_map/ppermute | solution.py:221
  211.5 0.0 slice-done.3
  211.5 4.3 %gram_stage.7.refs_0_ = f32[768,768]{1,0:T(8,128)S(1)} custom-call(bf16[1536,768]{1,0:T(8,128)(2,1)} %collective-permute-done.6.refs_0_.refs_10_, bf16[3840,768]{1,0:T(8,128)(2,1)S(1)} %bitcast.25), custom_call_target="tpu_custom_call" | custom-call | flops 1811939328 | tf_op jit(solution)/shard_map/gram_stage/pallas_call | solution.py:71
  215.8 46.3 %collective-permute-done.5.refs_1_.refs_11_ = bf16[1536,768]{1,0:T(8,128)(2,1)} collective-permute-done((bf16[1536,768]{1,0:T(8,128)(2,1)}, bf16[1536,768]{1,0:T(8,128)(2,1)}, u32[]{:S(2)}, u32[]{:S(2)}) %collective-permute-start.5) | collective-permute-done | bytes 2359328 | tf_op jit(solution)/shard_map/ppermute | solution.py:221
  262.0 4.3 %gram_stage.8.refs_0_ = f32[768,768]{1,0:T(8,128)S(1)} custom-call(f32[768,768]{1,0:T(8,128)S(1)} %gram_stage.7.refs_0_, bf16[1536,768]{1,0:T(8,128)(2,1)} %collective-permute-done.5.refs_1_.refs_11_, bf16[3840,768]{1,0:T(8,128)(2,1)S(1)} %bitcast.26), custom_call_target="tpu_custom_call" | custom-call | flops 1811939328 | tf_op jit(solution)/shard_map/gram_stage/pallas_call | solution.py:71
  266.3 3.1 %collective-permute-done.4.refs_1_.refs_12_ = bf16[256,768]{1,0:T(8,128)(2,1)S(1)} collective-permute-done((bf16[256,768]{1,0:T(8,128)(2,1)}, bf16[256,768]{1,0:T(8,128)(2,1)S(1)}, u32[]{:S(2)}, u32[]{:S(2)}) %collective-permute-start.4) | collective-permute-done | bytes 393248 | tf_op jit(solution)/shard_map/ppermute | solution.py:221
  269.4 0.5 gram_stage.9.refs_0_
  269.9 0.1 collective-permute-start.9
  270.0 3.2 %collective-permute-start.10 = (bf16[256,768]{1,0:T(8,128)(2,1)S(1)}, bf16[256,768]{1,0:T(8,128)(2,1)S(1)}, u32[]{:S(2)}, u32[]{:S(2)}) collective-permute-start(bf16[256,768]{1,0:T(8,128)(2,1)S(1)} %get-tuple-element.22.refs_3_), channel_id=1, source_target_pairs={{0,24},{2,26},{4,28},{6,30},{24,0},{26,2},{28,4},{30,6},{1,25},{3,... | collective-permute-start | bytes 1179656 | tf_op jit(solution)/shard_map/ppermute | solution.py:221
  273.2 4.6 %collective-permute-start.12 = (bf16[256,768]{1,0:T(8,128)(2,1)S(1)}, bf16[256,768]{1,0:T(8,128)(2,1)S(1)}, u32[]{:S(2)}, u32[]{:S(2)}) collective-permute-start(bf16[256,768]{1,0:T(8,128)(2,1)S(1)} %get-tuple-element.23.refs_7_), channel_id=1, source_target_pairs={{0,24},{2,26},{4,28},{6,30},{24,0},{26,2},{28,4},{30,6},{1,25},{3,... | collective-permute-start | bytes 1179656 | tf_op jit(solution)/shard_map/ppermute | solution.py:221
  277.8 7.8 %collective-permute-done.10.refs_2_.refs_13_ = bf16[256,768]{1,0:T(8,128)(2,1)S(1)} collective-permute-done((bf16[256,768]{1,0:T(8,128)(2,1)S(1)}, bf16[256,768]{1,0:T(8,128)(2,1)S(1)}, u32[]{:S(2)}, u32[]{:S(2)}) %collective-permute-start.10) | collective-permute-done | bytes 393248 | tf_op jit(solution)/shard_map/ppermute | solution.py:221
  285.7 0.0 collective-permute-start.11
  285.7 7.9 %collective-permute-done.12.refs_6_.refs_14_ = bf16[256,768]{1,0:T(8,128)(2,1)S(1)} collective-permute-done((bf16[256,768]{1,0:T(8,128)(2,1)S(1)}, bf16[256,768]{1,0:T(8,128)(2,1)S(1)}, u32[]{:S(2)}, u32[]{:S(2)}) %collective-permute-start.12) | collective-permute-done | bytes 393248 | tf_op jit(solution)/shard_map/ppermute | solution.py:221
  293.6 0.0 collective-permute-start.13
  293.6 0.0 collective-permute-done.11.refs_4_
  293.6 1.7 collective-permute-done.13.refs_8_
  295.4 0.0 collective-permute-done.9.refs_1_
  295.4 12.1 %far_stage.1 = f32[23040,128]{1,0:T(8,128)} custom-call(f32[2]{0:T(128)S(1)} %pad_maximum_fusion.1.energy, f32[1,768]{1,0:T(1,128)S(1)} %reshape.15.virt_row, f32[768,768]{1,0:T(8,128)S(1)} %gram_stage.9.refs_0_, f32[768,768]{1,0:T(8,128)S(1)} %collective-permute-done.9.refs_1_, bf16[256,768]{1,0:T(8,128)(2,1)S(1)} %collective-permute-done.10.refs_2_.refs_13_, ...), custom_call_target="tpu_custom_call" | custom-call | flops 4529848320 | bytes 11796480 | tf_op jit(solution)/shard_map/far_stage/pallas_call | solution.py:153
  (15 shorter events, 0.0 us)
Async XLA Ops:
  0.0 131.6 %collective-permute-start = (bf16[3840,768]{1,0:T(8,128)(2,1)}, bf16[3840,768]{1,0:T(8,128)(2,1)S(1)}, u32[]{:S(2)}, u32[]{:S(2)}) collective-permute-start(bf16[3840,768]{1,0:T(8,128)(2,1)} %bitcast.17), channel_id=1, source_target_pairs={{0,8},{2,10},{4,12},{6,14},{8,16},{10,18},{12,20},{14,22},{16,24},... | collective-permute-start | bytes 17694728 | tf_op jit(solution)/shard_map/ppermute | solution.py:216
  5.3 130.7 %collective-permute-start.1 = (bf16[3840,768]{1,0:T(8,128)(2,1)}, bf16[3840,768]{1,0:T(8,128)(2,1)S(1)}, u32[]{:S(2)}, u32[]{:S(2)}) collective-permute-start(bf16[3840,768]{1,0:T(8,128)(2,1)} %bitcast.18), channel_id=1, source_target_pairs={{8,0},{10,2},{12,4},{14,6},{16,8},{18,10},{20,12},{22,14},{24,16},... | collective-permute-start | bytes 17694728 | tf_op jit(solution)/shard_map/ppermute | solution.py:217
  6.6 129.4 %slice-start = ((s8[5898240]{0:T(1024)(128)(4,1)}), s8[4194304]{0:T(1024)(128)(4,1)S(1)}, s32[]{:S(2)}) async-start(s8[5898240]{0:T(1024)(128)(4,1)} %bitcast.19), calls=%async_computation | async-start | bytes 8388608
  8.9 127.1 %slice-start.1 = ((s8[5898240]{0:T(1024)(128)(4,1)}), s8[1703936]{0:T(1024)(128)(4,1)S(1)}, s32[]{:S(2)}) async-start(s8[5898240]{0:T(1024)(128)(4,1)} %bitcast.19), calls=%async_computation.1 | async-start | bytes 3407872
  131.6 12.8 %copy-start = (bf16[3840,768]{1,0:T(8,128)(2,1)}, bf16[3840,768]{1,0:T(8,128)(2,1)S(1)}, u32[]{:S(2)}) copy-start(bf16[3840,768]{1,0:T(8,128)(2,1)S(1)} %collective-permute-done.refs_0_.refs_4_) | copy-start | bytes 17694724
  136.0 8.4 %copy-start.2 = (bf16[3840,768]{1,0:T(8,128)(2,1)}, bf16[3840,768]{1,0:T(8,128)(2,1)S(1)}, u32[]{:S(2)}) copy-start(bf16[3840,768]{1,0:T(8,128)(2,1)S(1)} %collective-permute-done.1.refs_0_.refs_5_) | copy-start | bytes 17694724
  144.4 18.5 %copy-start.4 = (f32[16]{0:T(128)S(1)}, f32[16]{0:T(128)}, u32[]{:S(2)}) copy-start(f32[16]{0:T(128)} %param.4) | copy-start | bytes 196
  144.4 21.8 %copy-start.5 = (f32[768]{0:T(1024)S(1)}, f32[768]{0:T(1024)}, u32[]{:S(2)}) copy-start(f32[768]{0:T(1024)} %param.5) | copy-start | bytes 9220
  144.4 27.4 %collective-permute-start.7 = (f32[768,768]{1,0:T(8,128)}, f32[768,768]{1,0:T(8,128)}, u32[]{:S(2)}, u32[]{:S(2)}) collective-permute-start(f32[768,768]{1,0:T(8,128)} %gram_stage.5.refs_0_), channel_id=1, source_target_pairs={{0,1},{1,0},{2,3},{3,2},{4,5},{5,4},{6,7},{7,6},{8,9},{9,8},{10,11... | collective-permute-start | bytes 7077896 | tf_op jit(solution)/shard_map/ppermute | solution.py:23
  144.4 67.0 %slice-start.2 = ((s8[5898240]{0:T(1024)(128)(4,1)}), s8[1703936]{0:T(1024)(128)(4,1)S(1)}, s32[]{:S(2)}) async-start(s8[5898240]{0:T(1024)(128)(4,1)} %bitcast.23), calls=%async_computation.2 | async-start | bytes 3407872
  152.9 18.9 %collective-permute-start.8 = (f32[768,768]{1,0:T(8,128)}, f32[768,768]{1,0:T(8,128)}, u32[]{:S(2)}, u32[]{:S(2)}) collective-permute-start(f32[768,768]{1,0:T(8,128)} %gram_stage.6.refs_2_), channel_id=1, source_target_pairs={{0,1},{1,0},{2,3},{3,2},{4,5},{5,4},{6,7},{7,6},{8,9},{9,8},{10,11... | collective-permute-start | bytes 7077896 | tf_op jit(solution)/shard_map/ppermute | solution.py:23
  153.3 58.1 %collective-permute-start.6 = (bf16[1536,768]{1,0:T(8,128)(2,1)}, bf16[1536,768]{1,0:T(8,128)(2,1)}, u32[]{:S(2)}, u32[]{:S(2)}) collective-permute-start(bf16[1536,768]{1,0:T(8,128)(2,1)} %get-tuple-element.27), channel_id=1, source_target_pairs={{0,24},{2,26},{4,28},{6,30},{24,0},{26,2},{28,4},{30,6},{1,25},{3,... | collective-permute-start | bytes 7077896 | tf_op jit(solution)/shard_map/ppermute | solution.py:221
  156.5 105.5 %collective-permute-start.5 = (bf16[1536,768]{1,0:T(8,128)(2,1)}, bf16[1536,768]{1,0:T(8,128)(2,1)}, u32[]{:S(2)}, u32[]{:S(2)}) collective-permute-start(bf16[1536,768]{1,0:T(8,128)(2,1)} %get-tuple-element.26), channel_id=1, source_target_pairs={{0,24},{2,26},{4,28},{6,30},{24,0},{26,2},{28,4},{30,6},{1,25},{3,... | collective-permute-start | bytes 7077896 | tf_op jit(solution)/shard_map/ppermute | solution.py:221
  161.0 1.8 collective-permute-start.2
  162.8 5.5 %collective-permute-start.3 = (bf16[256,768]{1,0:T(8,128)(2,1)S(1)}, bf16[256,768]{1,0:T(8,128)(2,1)S(1)}, u32[]{:S(2)}, u32[]{:S(2)}) collective-permute-start(bf16[256,768]{1,0:T(8,128)(2,1)S(1)} %get-tuple-element.23.refs_7_), channel_id=1, source_target_pairs={{0,1},{1,0},{2,3},{3,2},{4,5},{5,4},{6,7},{7,6},{8,9},{9,8},{10,11... | collective-permute-start | bytes 1179656 | tf_op jit(solution)/shard_map/ppermute | solution.py:23
  168.3 43.2 %slice-start.3 = ((s8[5898240]{0:T(1024)(128)(4,1)}), s8[4194304]{0:T(1024)(128)(4,1)S(1)}, s32[]{:S(2)}) async-start(s8[5898240]{0:T(1024)(128)(4,1)} %bitcast.23), calls=%async_computation.3 | async-start | bytes 8388608
  168.3 101.1 %collective-permute-start.4 = (bf16[256,768]{1,0:T(8,128)(2,1)}, bf16[256,768]{1,0:T(8,128)(2,1)S(1)}, u32[]{:S(2)}, u32[]{:S(2)}) collective-permute-start(bf16[256,768]{1,0:T(8,128)(2,1)} %get-tuple-element.25), channel_id=1, source_target_pairs={{0,24},{2,26},{4,28},{6,30},{24,0},{26,2},{28,4},{30,6},{1,25},{3,... | collective-permute-start | bytes 1179656 | tf_op jit(solution)/shard_map/ppermute | solution.py:221
  171.8 2.7 copy-start.1
  174.5 2.7 copy-start.3
  269.9 25.4 %collective-permute-start.9 = (f32[768,768]{1,0:T(8,128)S(1)}, f32[768,768]{1,0:T(8,128)S(1)}, u32[]{:S(2)}, u32[]{:S(2)}) collective-permute-start(f32[768,768]{1,0:T(8,128)S(1)} %gram_stage.9.refs_0_), channel_id=1, source_target_pairs={{0,1},{1,0},{2,3},{3,2},{4,5},{5,4},{6,7},{7,6},{8,9},{9,8},{10,11... | collective-permute-start | bytes 7077896 | tf_op jit(solution)/shard_map/ppermute | solution.py:23
  270.0 15.7 %collective-permute-start.10 = (bf16[256,768]{1,0:T(8,128)(2,1)S(1)}, bf16[256,768]{1,0:T(8,128)(2,1)S(1)}, u32[]{:S(2)}, u32[]{:S(2)}) collective-permute-start(bf16[256,768]{1,0:T(8,128)(2,1)S(1)} %get-tuple-element.22.refs_3_), channel_id=1, source_target_pairs={{0,24},{2,26},{4,28},{6,30},{24,0},{26,2},{28,4},{30,6},{1,25},{3,... | collective-permute-start | bytes 1179656 | tf_op jit(solution)/shard_map/ppermute | solution.py:221
  273.2 20.4 %collective-permute-start.12 = (bf16[256,768]{1,0:T(8,128)(2,1)S(1)}, bf16[256,768]{1,0:T(8,128)(2,1)S(1)}, u32[]{:S(2)}, u32[]{:S(2)}) collective-permute-start(bf16[256,768]{1,0:T(8,128)(2,1)S(1)} %get-tuple-element.23.refs_7_), channel_id=1, source_target_pairs={{0,24},{2,26},{4,28},{6,30},{24,0},{26,2},{28,4},{30,6},{1,25},{3,... | collective-permute-start | bytes 1179656 | tf_op jit(solution)/shard_map/ppermute | solution.py:221
  285.7 7.9 %collective-permute-start.11 = (bf16[256,768]{1,0:T(8,128)(2,1)S(1)}, bf16[256,768]{1,0:T(8,128)(2,1)S(1)}, u32[]{:S(2)}, u32[]{:S(2)}) collective-permute-start(bf16[256,768]{1,0:T(8,128)(2,1)S(1)} %collective-permute-done.10.refs_2_.refs_13_), channel_id=1, source_target_pairs={{0,1},{1,0},{2,3},{3,2},{4,5},{5,4},{6,7},{7,6},{8,9},{9,8},{10,11... | collective-permute-start | bytes 1179656 | tf_op jit(solution)/shard_map/ppermute | solution.py:23
  293.6 1.7 collective-permute-start.13

commit v2 on v1

--- a/solution.py
+++ b/solution.py
@@ -10,6 +10,9 @@
 
 
 LANES = 128
+NEAR_SHARES = (24, 204, 12)
+FAR_SHARES = (96, 96, 21, 15, 12)
+NEAR_VMEM = 18 << 20
 F32 = jnp.float32
 BF16 = jnp.bfloat16
 ROWS_IN = (((0,), (0,)), ((), ()))
@@ -39,13 +42,14 @@
 
 def fill_tilde(tilde, amp, sums, pairs, across, e_left, e_right):
     width = tilde.shape[0]
+    for left, right in pairs:
+        amp[...] = gram(left[...], right[...])
+        sums = [*sums, amp]
     for at in range(0, width, LANES):
         here = pl.ds(at, LANES)
         whole = sums[0][here, :]
         for other in sums[1:]:
             whole = whole + other[here, :]
-        for left, right in pairs:
-            whole = whole + gram(left[:, at : at + LANES], right[...])
         down = jnp.transpose(jnp.broadcast_to(across[:, at : at + LANES], (LANES, LANES)))
         amp[here, :] = whole / (down[:, :1] + across - e_left - e_right)
     for at in range(0, width, LANES):
@@ -79,31 +83,41 @@
     )(*[on_chip(value) for value in operands])
 
 
-def near_kernel(block, n_sums, energy, virt_row, *refs):
-    sums, (behind, ahead, out, amp, *tildes) = refs[: 2 * n_sums], refs[2 * n_sums :]
+def near_kernel(n_sums, heights, energy, virt_row, *refs):
+    sums, refs = refs[: 2 * n_sums], refs[2 * n_sums :]
+    behind, ahead = refs[: len(heights)], refs[len(heights) : 2 * len(heights)]
+    out, amp, *tildes = refs[2 * len(heights) :]
     across = virt_row[...]
     for item, tilde in enumerate(tildes):
         terms = sums[item * n_sums : (item + 1) * n_sums]
         fill_tilde(tilde, amp, terms, [], across, energy[2 * item], energy[2 * item + 1])
 
-    @pl.loop(0, out.shape[0] // block)
-    def _(step):
-        here = pl.ds(pl.multiple_of(step * block, block), block)
-        first = jnp.dot(behind[here, :], tildes[0][...], preferred_element_type=F32)
-        out[here, :] = first + jnp.dot(ahead[here, :], tildes[1][...], preferred_element_type=F32)
-
-
-def near_stage(energy, virt_row, sums, behind, ahead, block):
-    rows, width = behind.shape
+    first = 0
+    for height, left, right in zip(heights, behind, ahead):
+        block = largest_block(height, 640)
+
+        @pl.loop(0, height // block)
+        def _(step, first=first, block=block, left=left, right=right):
+            here = pl.ds(pl.multiple_of(step * block, block), block)
+            there = pl.ds(pl.multiple_of(first + step * block, math.gcd(first, block)), block)
+            term = jnp.dot(left[here, :], tildes[0][...], preferred_element_type=F32)
+            out[there, :] = term + jnp.dot(right[here, :], tildes[1][...], preferred_element_type=F32)
+
+        first += height
+
+
+def near_stage(energy, virt_row, sums, behind, ahead):
+    heights = tuple(part.shape[0] for part in behind)
+    rows, width = sum(heights), behind[0].shape[1]
     vmem = pl.BlockSpec(memory_space=pltpu.VMEM)
-    operands = [virt_row, *sums, behind, ahead]
+    operands = [virt_row, *sums, *behind, *ahead]
     return pl.pallas_call(
-        functools.partial(near_kernel, block, len(sums) // 2),
+        functools.partial(near_kernel, len(sums) // 2, heights),
         in_specs=[pl.BlockSpec(memory_space=pltpu.SMEM)] + [vmem] * len(operands),
         out_specs=vmem,
         out_shape=pltpu.VMEM((rows, width), F32),
         scratch_shapes=[pltpu.VMEM((width, width), F32)] + [pltpu.VMEM((width, width), BF16)] * 2,
-        compiler_params=pltpu.CompilerParams(vmem_limit_bytes=16 << 20),
+        compiler_params=pltpu.CompilerParams(vmem_limit_bytes=NEAR_VMEM),
         cost_estimate=pl.CostEstimate(flops=4 * rows * width * width, bytes_accessed=0, transcendentals=0),
         name="near_stage",
     )(energy, *[on_chip(value) for value in operands])
@@ -190,11 +204,26 @@
     return total
 
 
-def far_cuts(rows, unit):
-    steps = rows // unit
-    if lax.axis_size("aux") != 2 or steps < 4:
-        return [0, rows], 0
-    return [0, (steps * 2 // 5) * unit, (steps * 4 // 5) * unit, (steps - 2) * unit, (steps - 1) * unit, rows], 2
+def cuts_of(rows, shares):
+    unit, rest = divmod(rows, sum(shares))
+    if rest or unit % 16:
+        return [0, rows]
+    return [unit * sum(shares[:at]) for at in range(len(shares) + 1)]
+
+
+def sent(pieces, ring):
+    arrived = []
+    for piece in pieces:
+        arrived.append(lax.ppermute(piece, "occ", ring))
+    return arrived
+
+
+def grams_of(parts, own, cuts, start=None):
+    for part, at in zip(parts, cuts):
+        if start is not None:
+            part, start = lax.optimization_barrier((part, start))
+        start = gram_stage(part, own, at, start)
+    return start
 
 
 def local(factors, occ_energy, virt_energy):
@@ -204,7 +233,11 @@
         return plain(factors, occ_energy, virt_energy)
     offset = n_blocks // 4
     index = lax.axis_index("occ")
-    cuts, n_late = far_cuts(rows, largest_block(rows, 256))
+    near_cuts, far_cuts, n_late = [0, rows], [0, rows], 0
+    if lax.axis_size("aux") == 2:
+        near_cuts = cuts_of(rows, NEAR_SHARES)
+        far_cuts = cuts_of(rows, FAR_SHARES)
+        n_late = int(len(far_cuts) > 2)
 
     up = [(s, s + offset) for s in range(n_blocks - offset)]
     down = [(s + offset, s) for s in range(n_blocks - offset)]
@@ -212,13 +245,14 @@
     ends = ends + [(t, s) for s, t in ends]
 
     own = factors.reshape(rows, width)
-    pieces = [own[a:b] for a, b in zip(cuts[:-1], cuts[1:])]
-    behind = lax.ppermute(own, "occ", up)
-    ahead = lax.ppermute(own, "occ", down)
-    *pieces, behind, ahead = lax.optimization_barrier((*pieces, behind, ahead))
-    far = []
-    for piece in pieces:
-        far.append(lax.ppermute(piece, "occ", ends))
+    pieces = [own[a:b] for a, b in zip(near_cuts[:-1], near_cuts[1:])]
+    behind, ahead = sent(pieces, up), sent(pieces, down)
+
+    pieces = [own[a:b] for a, b in zip(far_cuts[:-1], far_cuts[1:])]
+    at = max(0, len(behind) - 2)
+    pieces[0], behind[at], ahead[at] = lax.optimization_barrier((pieces[0], behind[at], ahead[at]))
+    *pieces[1:], behind[-1], ahead[-1] = lax.optimization_barrier((*pieces[1:], behind[-1], ahead[-1]))
+    far = sent(pieces, ends)
 
     e_own = occ_energy[index]
     e_ahead = occ_energy[(index + offset) % n_blocks]
@@ -230,21 +264,19 @@
     far_energy = jnp.stack([jnp.where(last, e_own, e_behind), jnp.where(last, e_ahead, e_own)])
     others = [swapped(piece) for piece in pieces[len(pieces) - n_late :]]
     energy, far_energy, *others = lax.optimization_barrier((energy, far_energy, *others))
-    grams = [gram_stage(behind, own), gram_stage(ahead, own)]
+    grams = [grams_of(parts[:-1], own, near_cuts) for parts in (behind, ahead)]
+    close = [grams_of(parts[-1:], own, near_cuts[-2:-1], start) for parts, start in zip((behind, ahead), grams)]
+    grams = close
     sums = aux_terms(grams[0]) + aux_terms(grams[1])
-    base = near_stage(energy, virt_row, sums, behind, ahead, largest_block(rows, 480))
+    base = near_stage(energy, virt_row, sums, behind, ahead)
 
     far[0], base = lax.optimization_barrier((far[0], base))
-    early = None
-    for part, at in list(zip(far, cuts))[: len(far) - n_late]:
-        if early is not None:
-            part, early = lax.optimization_barrier((part, early))
-        early = gram_stage(part, own, at, early)
-    sums = aux_terms(early)
+    sums = aux_terms(grams_of(far[: len(far) - n_late], own, far_cuts))
     pairs = []
-    for part, piece, other in zip(far[len(far) - n_late :], pieces[len(far) - n_late :], others):
-        pairs += [(part, piece), (swapped(part), other)]
-    out = far_stage(far_energy, virt_row, sums, pairs, far, base, largest_block(rows, 960))
+    if n_late:
+        pairs = [(swapped(far[-1]), others[0])]
+        sums[0] = gram_stage(far[-1], own, far_cuts[-2], sums[0])
+    out = far_stage(far_energy, virt_row, sums, pairs, far, base, min(rows, 768))
     return out.reshape(rows, count, width)
 
 

time: 308 us -> 320 us (1.039)
  starting transfers between devices: 26.3 us -> 38.7 us
    ppermute x7 -> x11, starting transfers between devices: 25.5 us -> 38.1 us  [sent(): arrived.append(lax.ppermute(piece, 'occ', ring))]
    pallas_call x5 -> x11, Pallas kernels: 25.9 us -> 29.9 us  [gram_stage(): pl.pallas_call(functools.partial(gram_kernel, largest_block(left.shape[0]...]
    ppermute x7 -> x11, waiting for transfers between devices: 205 us -> 205 us  [sent(): arrived.append(lax.ppermute(piece, 'occ', ring))]
    slice x2 -> x6, local copies, waits for them, and re-layouts: 7.3 us -> 7.8 us  [the longest x4 4.86 us: local(): pieces = [own[a:b] for a, b in zip(far_cuts[:-1], far_cuts[1:])]]
  transfers between devices with their start and end apart: 14 -> 16, of which waited for: 9 -> 7; matrix products, arithmetic and copies ran while one was open for 3% -> 2% of each run, Pallas kernels for 11% -> 11%
where the time goes in v2:
time: 320 us; the launch traced here: 319 us
  waiting for transfers between devices  206 us (64%)
  Pallas kernels  56.5 us (18%)
  starting transfers between devices  38.7 us (12%)
  local copies, waits for them, and re-layouts  13.3 us (4%)
    ppermute x11, waiting for transfers between devices, sent(): arrived.append(lax.ppermute(piece, 'occ', ring))  205 us
    ppermute x11, starting transfers between devices, sent(): arrived.append(lax.ppermute(piece, 'occ', ring))  38.1 us
    pallas_call x11, Pallas kernels, gram_stage(): pl.pallas_call(functools.partial(gram_kernel, largest_block(left.shape[0]...  29.9 us
    pallas_call x1, Pallas kernels, near_stage(): pl.pallas_call(functools.partial(near_kernel, len(sums) // 2, heights), i...  15.4 us
    pallas_call x1, Pallas kernels, far_stage(): pl.pallas_call(functools.partial(far_kernel, block, len(sums), len(pairs)...  11.2 us
  transfers between devices with their start and end apart: 16, of which 7 were waited for; matrix products, arithmetic and copies ran while one was open for 2% of the time, Pallas kernels for 11%

profile of v2, /device:TPU:0, one launch (start us, length us, event | category | flops | bytes accessed | tf_op | source)
XLA Modules:
  0.0 319.4 jit_solution(2845177324827452428)
XLA Ops:
  0.0 2.9 slice_bitcast_fusion
  2.9 5.4 %collective-permute-start.6 = (bf16[3264,768]{1,0:T(8,128)(2,1)S(1)}, bf16[3264,768]{1,0:T(8,128)(2,1)S(1)}, u32[]{:S(2)}, u32[]{:S(2)}) collective-permute-start(bf16[3264,768]{1,0:T(8,128)(2,1)S(1)} %slice_bitcast_fusion), channel_id=1, source_target_pairs={{0,8},{2,10},{4,12},{6,14},{8,16},{10,18},{12,20},{14,22},{16,24},... | collective-permute-start | bytes 15040520 | tf_op jit(solution)/shard_map/ppermute | solution.py:217
  8.3 1.3 collective-permute-start.7
  9.7 4.6 %collective-permute-start.9 = (bf16[384,768]{1,0:T(8,128)(2,1)S(1)}, bf16[384,768]{1,0:T(8,128)(2,1)S(1)}, u32[]{:S(2)}, u32[]{:S(2)}) collective-permute-start(bf16[384,768]{1,0:T(8,128)(2,1)S(1)} %slice_bitcast_fusion.3), channel_id=1, source_target_pairs={{0,8},{2,10},{4,12},{6,14},{8,16},{10,18},{12,20},{14,22},{16,24},... | collective-permute-start | bytes 1769480 | tf_op jit(solution)/shard_map/ppermute | solution.py:217
  14.3 1.3 collective-permute-start.11
  15.6 0.8 slice_bitcast_fusion.6
  16.3 4.6 %collective-permute-start = (bf16[192,768]{1,0:T(8,128)(2,1)}, bf16[192,768]{1,0:T(8,128)(2,1)S(1)}, u32[]{:S(2)}, u32[]{:S(2)}) collective-permute-start(bf16[192,768]{1,0:T(8,128)(2,1)} %slice_bitcast_fusion.6), channel_id=1, source_target_pairs={{0,8},{2,10},{4,12},{6,14},{8,16},{10,18},{12,20},{14,22},{16,24},... | collective-permute-start | bytes 884744 | tf_op jit(solution)/shard_map/ppermute | solution.py:217
  20.9 2.5 slice_bitcast_fusion.1
  23.4 111.1 %collective-permute-done.refs_1_.refs_6_ = bf16[192,768]{1,0:T(8,128)(2,1)S(1)} collective-permute-done((bf16[192,768]{1,0:T(8,128)(2,1)}, bf16[192,768]{1,0:T(8,128)(2,1)S(1)}, u32[]{:S(2)}, u32[]{:S(2)}) %collective-permute-start) | collective-permute-done | bytes 294944 | tf_op jit(solution)/shard_map/ppermute | solution.py:217
  134.4 1.3 collective-permute-start.1
  135.7 0.8 slice_bitcast_fusion.5
  136.5 0.8 slice_bitcast_fusion.4
  137.3 7.7 %collective-permute-done.1.refs_1_.refs_9_ = bf16[192,768]{1,0:T(8,128)(2,1)S(1)} collective-permute-done((bf16[192,768]{1,0:T(8,128)(2,1)}, bf16[192,768]{1,0:T(8,128)(2,1)S(1)}, u32[]{:S(2)}, u32[]{:S(2)}) %collective-permute-start.1) | collective-permute-done | bytes 294944 | tf_op jit(solution)/shard_map/ppermute | solution.py:217
  145.1 0.8 gram_stage.11.refs_0_
  145.9 0.8 gram_stage.14.refs_0_
  146.7 0.0 copy-start.1
  146.7 7.0 %gram_stage.12.refs_0_ = f32[768,768]{1,0:T(8,128)S(1)} custom-call(f32[768,768]{1,0:T(8,128)S(1)} %gram_stage.11.refs_0_, bf16[3264,768]{1,0:T(8,128)(2,1)S(1)} %collective-permute-done.6.refs_1_.refs_5_, bf16[3840,768]{1,0:T(8,128)(2,1)S(1)} %bitcast.23), custom_call_target="tpu_custom_call" | custom-call | flops 3850371072 | tf_op jit(solution)/shard_map/gram_stage/pallas_call | solution.py:75
  153.7 1.9 gram_stage.13.refs_0_
  155.6 6.9 %gram_stage.15.refs_0_ = f32[768,768]{1,0:T(8,128)S(1)} custom-call(f32[768,768]{1,0:T(8,128)S(1)} %gram_stage.14.refs_0_, bf16[3264,768]{1,0:T(8,128)(2,1)S(1)} %collective-permute-done.7.refs_1_.refs_8_, bf16[3840,768]{1,0:T(8,128)(2,1)S(1)} %bitcast.25), custom_call_target="tpu_custom_call" | custom-call | flops 3850371072 | tf_op jit(solution)/shard_map/gram_stage/pallas_call | solution.py:75
  162.6 0.0 copy-start.5
  162.6 0.0 copy-start.6
  162.6 0.0 slice-start
  162.6 2.0 gram_stage.16.refs_2_
  164.6 0.5 collective-permute-start.12
  165.1 3.7 %collective-permute-start.8 = (bf16[1536,768]{1,0:T(8,128)(2,1)}, bf16[1536,768]{1,0:T(8,128)(2,1)}, u32[]{:S(2)}, u32[]{:S(2)}) collective-permute-start(bf16[1536,768]{1,0:T(8,128)(2,1)} %get-tuple-element.38), channel_id=1, source_target_pairs={{0,24},{2,26},{4,28},{6,30},{24,0},{26,2},{28,4},{30,6},{1,25},{3,... | collective-permute-start | bytes 7077896 | tf_op jit(solution)/shard_map/ppermute | solution.py:217
  168.8 3.9 %collective-permute-start.5 = (bf16[1536,768]{1,0:T(8,128)(2,1)}, bf16[1536,768]{1,0:T(8,128)(2,1)}, u32[]{:S(2)}, u32[]{:S(2)}) collective-permute-start(bf16[1536,768]{1,0:T(8,128)(2,1)} %get-tuple-element.37), channel_id=1, source_target_pairs={{0,24},{2,26},{4,28},{6,30},{24,0},{26,2},{28,4},{30,6},{1,25},{3,... | collective-permute-start | bytes 7077896 | tf_op jit(solution)/shard_map/ppermute | solution.py:217
  172.8 0.1 collective-permute-start.2
  172.9 0.7 fusion
  176.1 2.0 pad_maximum_fusion.energy
  178.1 0.1 pad_maximum_fusion.1.energy
  178.2 4.0 %collective-permute-start.3 = (bf16[240,768]{1,0:T(8,128)(2,1)}, bf16[240,768]{1,0:T(8,128)(2,1)S(1)}, u32[]{:S(2)}, u32[]{:S(2)}) collective-permute-start(bf16[240,768]{1,0:T(8,128)(2,1)} %slice_bitcast_fusion.5), channel_id=1, source_target_pairs={{0,24},{2,26},{4,28},{6,30},{24,0},{26,2},{28,4},{30,6},{1,25},{3,... | collective-permute-start | bytes 1105928 | tf_op jit(solution)/shard_map/ppermute | solution.py:217
  182.2 4.1 %collective-permute-start.4 = (bf16[336,768]{1,0:T(8,128)(2,1)}, bf16[336,768]{1,0:T(8,128)(2,1)S(1)}, u32[]{:S(2)}, u32[]{:S(2)}) collective-permute-start(bf16[336,768]{1,0:T(8,128)(2,1)} %slice_bitcast_fusion.4), channel_id=1, source_target_pairs={{0,24},{2,26},{4,28},{6,30},{24,0},{26,2},{28,4},{30,6},{1,25},{3,... | collective-permute-start | bytes 1548296 | tf_op jit(solution)/shard_map/ppermute | solution.py:217
  186.3 2.4 copy-done.2
  188.7 2.4 copy-done.4
  191.2 15.4 %near_stage.1.refs_9_ = f32[3840,768]{1,0:T(8,128)S(1)} custom-call(f32[4]{0:T(128)S(1)} %pad_maximum_fusion.energy, f32[1,768]{1,0:T(1,128)S(1)} %reshape.16.virt_row, f32[768,768]{1,0:T(8,128)} %gram_stage.13.refs_0_, f32[768,768]{1,0:T(8,128)} %collective-permute-done.10.refs_1_, f32[768,768]{1,0:T(8,128)} %gram_stage.16.refs_2_, ...), custom_call_target="tpu_custom_call" | custom-call | flops 9059696640 | tf_op jit(solution)/shard_map/near_stage/pallas_call | solution.py:114
  206.5 16.7 %collective-permute-done.8.refs_0_.refs_4_ = bf16[1536,768]{1,0:T(8,128)(2,1)} collective-permute-done((bf16[1536,768]{1,0:T(8,128)(2,1)}, bf16[1536,768]{1,0:T(8,128)(2,1)}, u32[]{:S(2)}, u32[]{:S(2)}) %collective-permute-start.8) | collective-permute-done | bytes 2359328 | tf_op jit(solution)/shard_map/ppermute | solution.py:217
  223.2 4.3 %gram_stage.17.refs_0_ = f32[768,768]{1,0:T(8,128)S(1)} custom-call(bf16[1536,768]{1,0:T(8,128)(2,1)} %collective-permute-done.8.refs_0_.refs_4_, bf16[3840,768]{1,0:T(8,128)(2,1)S(1)} %bitcast.29), custom_call_target="tpu_custom_call" | custom-call | flops 1811939328 | tf_op jit(solution)/shard_map/gram_stage/pallas_call | solution.py:75
  227.5 46.3 %collective-permute-done.5.refs_1_.refs_5_ = bf16[1536,768]{1,0:T(8,128)(2,1)} collective-permute-done((bf16[1536,768]{1,0:T(8,128)(2,1)}, bf16[1536,768]{1,0:T(8,128)(2,1)}, u32[]{:S(2)}, u32[]{:S(2)}) %collective-permute-start.5) | collective-permute-done | bytes 2359328 | tf_op jit(solution)/shard_map/ppermute | solution.py:217
  273.8 4.3 %gram_stage.18.refs_0_ = f32[768,768]{1,0:T(8,128)S(1)} custom-call(f32[768,768]{1,0:T(8,128)S(1)} %gram_stage.17.refs_0_, bf16[1536,768]{1,0:T(8,128)(2,1)} %collective-permute-done.5.refs_1_.refs_5_, bf16[3840,768]{1,0:T(8,128)(2,1)S(1)} %bitcast.30), custom_call_target="tpu_custom_call" | custom-call | flops 1811939328 | tf_op jit(solution)/shard_map/gram_stage/pallas_call | solution.py:75
  278.1 13.6 %collective-permute-done.4.refs_1_.refs_6_ = bf16[336,768]{1,0:T(8,128)(2,1)S(1)} collective-permute-done((bf16[336,768]{1,0:T(8,128)(2,1)}, bf16[336,768]{1,0:T(8,128)(2,1)S(1)}, u32[]{:S(2)}, u32[]{:S(2)}) %collective-permute-start.4) | collective-permute-done | bytes 516128 | tf_op jit(solution)/shard_map/ppermute | solution.py:217
  291.7 0.8 gram_stage.19.refs_0_
  292.5 0.5 gram_stage.20.refs_0_
  293.0 0.1 collective-permute-start.14
  293.1 4.0 %collective-permute-start.13 = (bf16[192,768]{1,0:T(8,128)(2,1)}, bf16[192,768]{1,0:T(8,128)(2,1)S(1)}, u32[]{:S(2)}, u32[]{:S(2)}) collective-permute-start(bf16[192,768]{1,0:T(8,128)(2,1)} %slice_bitcast_fusion.6), channel_id=1, source_target_pairs={{0,24},{2,26},{4,28},{6,30},{24,0},{26,2},{28,4},{30,6},{1,25},{3,... | collective-permute-start | bytes 884744 | tf_op jit(solution)/shard_map/ppermute | solution.py:217
  297.1 9.3 %collective-permute-done.13.refs_1_.refs_8_ = bf16[192,768]{1,0:T(8,128)(2,1)S(1)} collective-permute-done((bf16[192,768]{1,0:T(8,128)(2,1)}, bf16[192,768]{1,0:T(8,128)(2,1)S(1)}, u32[]{:S(2)}, u32[]{:S(2)}) %collective-permute-start.13) | collective-permute-done | bytes 294944 | tf_op jit(solution)/shard_map/ppermute | solution.py:217
  306.4 0.5 gram_stage.21.refs_0_
  307.0 1.0 collective-permute-done.15.refs_2_
  308.0 11.2 %far_stage.1 = f32[23040,128]{1,0:T(8,128)} custom-call(f32[2]{0:T(128)S(1)} %pad_maximum_fusion.1.energy, f32[1,768]{1,0:T(1,128)S(1)} %reshape.16.virt_row, f32[768,768]{1,0:T(8,128)S(1)} %gram_stage.21.refs_0_, f32[768,768]{1,0:T(8,128)S(1)} %collective-permute-done.14.refs_1_, bf16[192,768]{1,0:T(8,128)(2,1)S(1)} %collective-permute-done.15.refs_2_, ...), custom_call_target="tpu_custom_call" | custom-call | flops 4529848320 | bytes 11796480 | tf_op jit(solution)/shard_map/far_stage/pallas_call | solution.py:167
  (26 shorter events, 0.1 us)
Async XLA Ops:
  0.0 9.6 %copy-start = (bf16[3840,1,768]{2,0,1:T(8,128)(2,1)S(1)}, bf16[3840,1,768]{2,0,1:T(8,128)(2,1)}, u32[]{:S(2)}) copy-start(bf16[3840,1,768]{2,0,1:T(8,128)(2,1)} %param.3) | copy-start | bytes 17694724
  2.9 143.8 %collective-permute-start.6 = (bf16[3264,768]{1,0:T(8,128)(2,1)S(1)}, bf16[3264,768]{1,0:T(8,128)(2,1)S(1)}, u32[]{:S(2)}, u32[]{:S(2)}) collective-permute-start(bf16[3264,768]{1,0:T(8,128)(2,1)S(1)} %slice_bitcast_fusion), channel_id=1, source_target_pairs={{0,8},{2,10},{4,12},{6,14},{8,16},{10,18},{12,20},{14,22},{16,24},... | collective-permute-start | bytes 15040520 | tf_op jit(solution)/shard_map/ppermute | solution.py:217
  8.3 138.4 %collective-permute-start.7 = (bf16[3264,768]{1,0:T(8,128)(2,1)S(1)}, bf16[3264,768]{1,0:T(8,128)(2,1)S(1)}, u32[]{:S(2)}, u32[]{:S(2)}) collective-permute-start(bf16[3264,768]{1,0:T(8,128)(2,1)S(1)} %slice_bitcast_fusion), channel_id=1, source_target_pairs={{8,0},{10,2},{12,4},{14,6},{16,8},{18,10},{20,12},{22,14},{24,16},... | collective-permute-start | bytes 15040520 | tf_op jit(solution)/shard_map/ppermute | solution.py:217
  9.7 135.4 %collective-permute-start.9 = (bf16[384,768]{1,0:T(8,128)(2,1)S(1)}, bf16[384,768]{1,0:T(8,128)(2,1)S(1)}, u32[]{:S(2)}, u32[]{:S(2)}) collective-permute-start(bf16[384,768]{1,0:T(8,128)(2,1)S(1)} %slice_bitcast_fusion.3), channel_id=1, source_target_pairs={{0,8},{2,10},{4,12},{6,14},{8,16},{10,18},{12,20},{14,22},{16,24},... | collective-permute-start | bytes 1769480 | tf_op jit(solution)/shard_map/ppermute | solution.py:217
  14.3 131.6 %collective-permute-start.11 = (bf16[384,768]{1,0:T(8,128)(2,1)S(1)}, bf16[384,768]{1,0:T(8,128)(2,1)S(1)}, u32[]{:S(2)}, u32[]{:S(2)}) collective-permute-start(bf16[384,768]{1,0:T(8,128)(2,1)S(1)} %slice_bitcast_fusion.3), channel_id=1, source_target_pairs={{8,0},{10,2},{12,4},{14,6},{16,8},{18,10},{20,12},{22,14},{24,16},... | collective-permute-start | bytes 1769480 | tf_op jit(solution)/shard_map/ppermute | solution.py:217
  16.3 118.1 %collective-permute-start = (bf16[192,768]{1,0:T(8,128)(2,1)}, bf16[192,768]{1,0:T(8,128)(2,1)S(1)}, u32[]{:S(2)}, u32[]{:S(2)}) collective-permute-start(bf16[192,768]{1,0:T(8,128)(2,1)} %slice_bitcast_fusion.6), channel_id=1, source_target_pairs={{0,8},{2,10},{4,12},{6,14},{8,16},{10,18},{12,20},{14,22},{16,24},... | collective-permute-start | bytes 884744 | tf_op jit(solution)/shard_map/ppermute | solution.py:217
  134.4 10.6 %collective-permute-start.1 = (bf16[192,768]{1,0:T(8,128)(2,1)}, bf16[192,768]{1,0:T(8,128)(2,1)S(1)}, u32[]{:S(2)}, u32[]{:S(2)}) collective-permute-start(bf16[192,768]{1,0:T(8,128)(2,1)} %slice_bitcast_fusion.6), channel_id=1, source_target_pairs={{8,0},{10,2},{12,4},{14,6},{16,8},{18,10},{20,12},{22,14},{24,16},... | collective-permute-start | bytes 884744 | tf_op jit(solution)/shard_map/ppermute | solution.py:217
  146.7 7.0 %copy-start.1 = (bf16[3264,768]{1,0:T(8,128)(2,1)}, bf16[3264,768]{1,0:T(8,128)(2,1)S(1)}, u32[]{:S(2)}) copy-start(bf16[3264,768]{1,0:T(8,128)(2,1)S(1)} %collective-permute-done.6.refs_1_.refs_5_) | copy-start | bytes 15040516
  146.7 8.9 %copy-start.3 = (bf16[3264,768]{1,0:T(8,128)(2,1)}, bf16[3264,768]{1,0:T(8,128)(2,1)S(1)}, u32[]{:S(2)}) copy-start(bf16[3264,768]{1,0:T(8,128)(2,1)S(1)} %collective-permute-done.7.refs_1_.refs_8_) | copy-start | bytes 15040516
  155.6 26.6 %collective-permute-start.10 = (f32[768,768]{1,0:T(8,128)}, f32[768,768]{1,0:T(8,128)}, u32[]{:S(2)}, u32[]{:S(2)}) collective-permute-start(f32[768,768]{1,0:T(8,128)} %gram_stage.13.refs_0_), channel_id=1, source_target_pairs={{0,1},{1,0},{2,3},{3,2},{4,5},{5,4},{6,7},{7,6},{8,9},{9,8},{10,11... | collective-permute-start | bytes 7077896 | tf_op jit(solution)/shard_map/ppermute | solution.py:26
  162.6 10.3 %copy-start.5 = (f32[16]{0:T(128)S(1)}, f32[16]{0:T(128)}, u32[]{:S(2)}) copy-start(f32[16]{0:T(128)} %param.4) | copy-start | bytes 196
  162.6 13.5 %copy-start.6 = (f32[768]{0:T(1024)S(1)}, f32[768]{0:T(1024)}, u32[]{:S(2)}) copy-start(f32[768]{0:T(1024)} %param.5) | copy-start | bytes 9220
  162.6 60.6 %slice-start = ((s8[5898240]{0:T(1024)(128)(4,1)}), s8[1703936]{0:T(1024)(128)(4,1)S(1)}, s32[]{:S(2)}) async-start(s8[5898240]{0:T(1024)(128)(4,1)} %bitcast.27), calls=%async_computation | async-start | bytes 3407872
  164.6 21.7 %collective-permute-start.12 = (f32[768,768]{1,0:T(8,128)}, f32[768,768]{1,0:T(8,128)}, u32[]{:S(2)}, u32[]{:S(2)}) collective-permute-start(f32[768,768]{1,0:T(8,128)} %gram_stage.16.refs_2_), channel_id=1, source_target_pairs={{0,1},{1,0},{2,3},{3,2},{4,5},{5,4},{6,7},{7,6},{8,9},{9,8},{10,11... | collective-permute-start | bytes 7077896 | tf_op jit(solution)/shard_map/ppermute | solution.py:26
  165.1 58.1 %collective-permute-start.8 = (bf16[1536,768]{1,0:T(8,128)(2,1)}, bf16[1536,768]{1,0:T(8,128)(2,1)}, u32[]{:S(2)}, u32[]{:S(2)}) collective-permute-start(bf16[1536,768]{1,0:T(8,128)(2,1)} %get-tuple-element.38), channel_id=1, source_target_pairs={{0,24},{2,26},{4,28},{6,30},{24,0},{26,2},{28,4},{30,6},{1,25},{3,... | collective-permute-start | bytes 7077896 | tf_op jit(solution)/shard_map/ppermute | solution.py:217
  168.8 104.9 %collective-permute-start.5 = (bf16[1536,768]{1,0:T(8,128)(2,1)}, bf16[1536,768]{1,0:T(8,128)(2,1)}, u32[]{:S(2)}, u32[]{:S(2)}) collective-permute-start(bf16[1536,768]{1,0:T(8,128)(2,1)} %get-tuple-element.37), channel_id=1, source_target_pairs={{0,24},{2,26},{4,28},{6,30},{24,0},{26,2},{28,4},{30,6},{1,25},{3,... | collective-permute-start | bytes 7077896 | tf_op jit(solution)/shard_map/ppermute | solution.py:217
  172.8 5.5 %collective-permute-start.2 = (bf16[192,768]{1,0:T(8,128)(2,1)}, bf16[192,768]{1,0:T(8,128)(2,1)}, u32[]{:S(2)}, u32[]{:S(2)}) collective-permute-start(bf16[192,768]{1,0:T(8,128)(2,1)} %slice_bitcast_fusion.6), channel_id=1, source_target_pairs={{0,1},{1,0},{2,3},{3,2},{4,5},{5,4},{6,7},{7,6},{8,9},{9,8},{10,11... | collective-permute-start | bytes 884744 | tf_op jit(solution)/shard_map/ppermute | solution.py:26
  178.2 45.0 %slice-start.1 = ((s8[5898240]{0:T(1024)(128)(4,1)}), s8[4194304]{0:T(1024)(128)(4,1)S(1)}, s32[]{:S(2)}) async-start(s8[5898240]{0:T(1024)(128)(4,1)} %bitcast.27), calls=%async_computation.1 | async-start | bytes 8388608
  178.2 114.3 %collective-permute-start.3 = (bf16[240,768]{1,0:T(8,128)(2,1)}, bf16[240,768]{1,0:T(8,128)(2,1)S(1)}, u32[]{:S(2)}, u32[]{:S(2)}) collective-permute-start(bf16[240,768]{1,0:T(8,128)(2,1)} %slice_bitcast_fusion.5), channel_id=1, source_target_pairs={{0,24},{2,26},{4,28},{6,30},{24,0},{26,2},{28,4},{30,6},{1,25},{3,... | collective-permute-start | bytes 1105928 | tf_op jit(solution)/shard_map/ppermute | solution.py:217
  182.2 109.5 %collective-permute-start.4 = (bf16[336,768]{1,0:T(8,128)(2,1)}, bf16[336,768]{1,0:T(8,128)(2,1)S(1)}, u32[]{:S(2)}, u32[]{:S(2)}) collective-permute-start(bf16[336,768]{1,0:T(8,128)(2,1)} %slice_bitcast_fusion.4), channel_id=1, source_target_pairs={{0,24},{2,26},{4,28},{6,30},{24,0},{26,2},{28,4},{30,6},{1,25},{3,... | collective-permute-start | bytes 1548296 | tf_op jit(solution)/shard_map/ppermute | solution.py:217
  186.3 2.4 copy-start.2
  188.7 2.4 copy-start.4
  293.0 15.0 %collective-permute-start.14 = (f32[768,768]{1,0:T(8,128)S(1)}, f32[768,768]{1,0:T(8,128)S(1)}, u32[]{:S(2)}, u32[]{:S(2)}) collective-permute-start(f32[768,768]{1,0:T(8,128)S(1)} %gram_stage.20.refs_0_), channel_id=1, source_target_pairs={{0,1},{1,0},{2,3},{3,2},{4,5},{5,4},{6,7},{7,6},{8,9},{9,8},{10,11... | collective-permute-start | bytes 7077896 | tf_op jit(solution)/shard_map/ppermute | solution.py:26
  293.1 13.3 %collective-permute-start.13 = (bf16[192,768]{1,0:T(8,128)(2,1)}, bf16[192,768]{1,0:T(8,128)(2,1)S(1)}, u32[]{:S(2)}, u32[]{:S(2)}) collective-permute-start(bf16[192,768]{1,0:T(8,128)(2,1)} %slice_bitcast_fusion.6), channel_id=1, source_target_pairs={{0,24},{2,26},{4,28},{6,30},{24,0},{26,2},{28,4},{30,6},{1,25},{3,... | collective-permute-start | bytes 884744 | tf_op jit(solution)/shard_map/ppermute | solution.py:217
  306.4 1.6 collective-permute-start.15

commit v3 on v2

--- a/solution.py
+++ b/solution.py
@@ -10,7 +10,7 @@
 
 
 LANES = 128
-NEAR_SHARES = (24, 204, 12)
+NEAR_SHARES = (24, 210, 6)
 FAR_SHARES = (96, 96, 21, 15, 12)
 NEAR_VMEM = 18 << 20
 F32 = jnp.float32
@@ -77,7 +77,7 @@
         in_specs=[vmem] * len(operands),
         out_specs=vmem,
         out_shape=pltpu.VMEM((width, width), F32),
-        compiler_params=pltpu.CompilerParams(vmem_limit_bytes=10 << 20),
+        compiler_params=pltpu.CompilerParams(vmem_limit_bytes=4 << 20),
         cost_estimate=pl.CostEstimate(flops=2 * left.size * width, bytes_accessed=0, transcendentals=0),
         name="gram_stage",
     )(*[on_chip(value) for value in operands])
@@ -175,7 +175,7 @@
             pltpu.VMEM((2, block * strips, LANES), F32),
             pltpu.SemaphoreType.DMA((2,)),
         ],
-        compiler_params=pltpu.CompilerParams(vmem_limit_bytes=20 << 20),
+        compiler_params=pltpu.CompilerParams(vmem_limit_bytes=14 << 20),
         cost_estimate=pl.CostEstimate(
             flops=2 * rows * width * width, bytes_accessed=4 * rows * width, transcendentals=0
         ),

time: 320 us -> 317 us (level)
  no operation moved by 1% of the time
where the time goes in v3:
time: 317 us; the launch traced here: 316 us
  waiting for transfers between devices  203 us (64%)
  Pallas kernels  56.5 us (18%)
  starting transfers between devices  38.9 us (12%)
  local copies, waits for them, and re-layouts  13.4 us (4%)
    ppermute x11, waiting for transfers between devices, sent(): arrived.append(lax.ppermute(piece, 'occ', ring))  201 us
    ppermute x11, starting transfers between devices, sent(): arrived.append(lax.ppermute(piece, 'occ', ring))  38.3 us
    pallas_call x11, Pallas kernels, gram_stage(): pl.pallas_call(functools.partial(gram_kernel, largest_block(left.shape[0]...  29.8 us
    pallas_call x1, Pallas kernels, near_stage(): pl.pallas_call(functools.partial(near_kernel, len(sums) // 2, heights), i...  15.5 us
    pallas_call x1, Pallas kernels, far_stage(): pl.pallas_call(functools.partial(far_kernel, block, len(sums), len(pairs)...  11.1 us
  transfers between devices with their start and end apart: 16, of which 7 were waited for; matrix products, arithmetic and copies ran while one was open for 2% of the time, Pallas kernels for 11%

profile of v3, /device:TPU:0, one launch (start us, length us, event | category | flops | bytes accessed | tf_op | source)
XLA Modules:
  0.0 316.1 jit_solution(2638834300374296390)
XLA Ops:
  0.0 2.9 slice_bitcast_fusion
  3.0 5.4 %collective-permute-start.6 = (bf16[3360,768]{1,0:T(8,128)(2,1)S(1)}, bf16[3360,768]{1,0:T(8,128)(2,1)S(1)}, u32[]{:S(2)}, u32[]{:S(2)}) collective-permute-start(bf16[3360,768]{1,0:T(8,128)(2,1)S(1)} %slice_bitcast_fusion), channel_id=1, source_target_pairs={{0,8},{2,10},{4,12},{6,14},{8,16},{10,18},{12,20},{14,22},{16,24},... | collective-permute-start | bytes 15482888 | tf_op jit(solution)/shard_map/ppermute | solution.py:217
  8.4 1.3 collective-permute-start.7
  9.7 4.6 %collective-permute-start.9 = (bf16[384,768]{1,0:T(8,128)(2,1)S(1)}, bf16[384,768]{1,0:T(8,128)(2,1)S(1)}, u32[]{:S(2)}, u32[]{:S(2)}) collective-permute-start(bf16[384,768]{1,0:T(8,128)(2,1)S(1)} %slice_bitcast_fusion.3), channel_id=1, source_target_pairs={{0,8},{2,10},{4,12},{6,14},{8,16},{10,18},{12,20},{14,22},{16,24},... | collective-permute-start | bytes 1769480 | tf_op jit(solution)/shard_map/ppermute | solution.py:217
  14.3 1.3 collective-permute-start.11
  15.6 4.6 %collective-permute-start = (bf16[96,768]{1,0:T(8,128)(2,1)S(1)}, bf16[96,768]{1,0:T(8,128)(2,1)S(1)}, u32[]{:S(2)}, u32[]{:S(2)}) collective-permute-start(bf16[96,768]{1,0:T(8,128)(2,1)S(1)} %slice_bitcast_fusion.7), channel_id=1, source_target_pairs={{0,8},{2,10},{4,12},{6,14},{8,16},{10,18},{12,20},{14,22},{16,24},... | collective-permute-start | bytes 442376 | tf_op jit(solution)/shard_map/ppermute | solution.py:217
  20.2 2.5 slice_bitcast_fusion.1
  22.7 0.8 slice_bitcast_fusion.4
  23.5 0.8 slice_bitcast_fusion.5
  24.3 110.1 %collective-permute-done.refs_1_.refs_6_ = bf16[96,768]{1,0:T(8,128)(2,1)S(1)} collective-permute-done((bf16[96,768]{1,0:T(8,128)(2,1)S(1)}, bf16[96,768]{1,0:T(8,128)(2,1)S(1)}, u32[]{:S(2)}, u32[]{:S(2)}) %collective-permute-start) | collective-permute-done | bytes 147488 | tf_op jit(solution)/shard_map/ppermute | solution.py:217
  134.4 1.3 collective-permute-start.1
  135.7 0.7 slice_bitcast_fusion.6
  136.4 5.5 %collective-permute-done.1.refs_1_.refs_9_ = bf16[96,768]{1,0:T(8,128)(2,1)S(1)} collective-permute-done((bf16[96,768]{1,0:T(8,128)(2,1)S(1)}, bf16[96,768]{1,0:T(8,128)(2,1)S(1)}, u32[]{:S(2)}, u32[]{:S(2)}) %collective-permute-start.1) | collective-permute-done | bytes 147488 | tf_op jit(solution)/shard_map/ppermute | solution.py:217
  141.9 0.8 gram_stage.11.refs_0_
  142.7 0.8 gram_stage.14.refs_0_
  143.5 0.0 copy-start.1
  143.6 7.0 %gram_stage.12.refs_0_ = f32[768,768]{1,0:T(8,128)S(1)} custom-call(f32[768,768]{1,0:T(8,128)S(1)} %gram_stage.11.refs_0_, bf16[3360,768]{1,0:T(8,128)(2,1)S(1)} %collective-permute-done.6.refs_1_.refs_5_, bf16[3840,768]{1,0:T(8,128)(2,1)S(1)} %bitcast.25), custom_call_target="tpu_custom_call" | custom-call | flops 3963617280 | tf_op jit(solution)/shard_map/gram_stage/pallas_call | solution.py:75
  150.6 1.9 gram_stage.13.refs_0_
  152.4 7.0 %gram_stage.15.refs_0_ = f32[768,768]{1,0:T(8,128)S(1)} custom-call(f32[768,768]{1,0:T(8,128)S(1)} %gram_stage.14.refs_0_, bf16[3360,768]{1,0:T(8,128)(2,1)S(1)} %collective-permute-done.7.refs_1_.refs_8_, bf16[3840,768]{1,0:T(8,128)(2,1)S(1)} %bitcast.27), custom_call_target="tpu_custom_call" | custom-call | flops 3963617280 | tf_op jit(solution)/shard_map/gram_stage/pallas_call | solution.py:75
  159.4 0.0 copy-start.5
  159.4 0.0 copy-start.6
  159.5 0.0 slice-start
  159.5 1.9 gram_stage.16.refs_2_
  161.4 0.5 collective-permute-start.12
  161.9 3.9 %collective-permute-start.8 = (bf16[1536,768]{1,0:T(8,128)(2,1)}, bf16[1536,768]{1,0:T(8,128)(2,1)}, u32[]{:S(2)}, u32[]{:S(2)}) collective-permute-start(bf16[1536,768]{1,0:T(8,128)(2,1)} %get-tuple-element.38), channel_id=1, source_target_pairs={{0,24},{2,26},{4,28},{6,30},{24,0},{26,2},{28,4},{30,6},{1,25},{3,... | collective-permute-start | bytes 7077896 | tf_op jit(solution)/shard_map/ppermute | solution.py:217
  165.8 3.7 %collective-permute-start.5 = (bf16[1536,768]{1,0:T(8,128)(2,1)}, bf16[1536,768]{1,0:T(8,128)(2,1)}, u32[]{:S(2)}, u32[]{:S(2)}) collective-permute-start(bf16[1536,768]{1,0:T(8,128)(2,1)} %get-tuple-element.37), channel_id=1, source_target_pairs={{0,24},{2,26},{4,28},{6,30},{24,0},{26,2},{28,4},{30,6},{1,25},{3,... | collective-permute-start | bytes 7077896 | tf_op jit(solution)/shard_map/ppermute | solution.py:217
  169.5 0.1 collective-permute-start.2
  169.7 0.6 fusion
  172.7 1.8 pad_maximum_fusion.energy
  174.5 0.1 pad_maximum_fusion.1.energy
  174.6 4.2 %collective-permute-start.3 = (bf16[240,768]{1,0:T(8,128)(2,1)}, bf16[240,768]{1,0:T(8,128)(2,1)S(1)}, u32[]{:S(2)}, u32[]{:S(2)}) collective-permute-start(bf16[240,768]{1,0:T(8,128)(2,1)} %slice_bitcast_fusion.5), channel_id=1, source_target_pairs={{0,24},{2,26},{4,28},{6,30},{24,0},{26,2},{28,4},{30,6},{1,25},{3,... | collective-permute-start | bytes 1105928 | tf_op jit(solution)/shard_map/ppermute | solution.py:217
  178.8 3.9 %collective-permute-start.4 = (bf16[336,768]{1,0:T(8,128)(2,1)}, bf16[336,768]{1,0:T(8,128)(2,1)S(1)}, u32[]{:S(2)}, u32[]{:S(2)}) collective-permute-start(bf16[336,768]{1,0:T(8,128)(2,1)} %slice_bitcast_fusion.4), channel_id=1, source_target_pairs={{0,24},{2,26},{4,28},{6,30},{24,0},{26,2},{28,4},{30,6},{1,25},{3,... | collective-permute-start | bytes 1548296 | tf_op jit(solution)/shard_map/ppermute | solution.py:217
  182.7 2.5 copy-done.2
  185.1 2.5 copy-done.4
  187.6 15.5 %near_stage.1.refs_9_ = f32[3840,768]{1,0:T(8,128)S(1)} custom-call(f32[4]{0:T(128)S(1)} %pad_maximum_fusion.energy, f32[1,768]{1,0:T(1,128)S(1)} %reshape.17.virt_row, f32[768,768]{1,0:T(8,128)} %gram_stage.13.refs_0_, f32[768,768]{1,0:T(8,128)} %collective-permute-done.10.refs_1_, f32[768,768]{1,0:T(8,128)} %gram_stage.16.refs_2_, ...), custom_call_target="tpu_custom_call" | custom-call | flops 9059696640 | tf_op jit(solution)/shard_map/near_stage/pallas_call | solution.py:114
  203.1 16.9 %collective-permute-done.8.refs_0_.refs_4_ = bf16[1536,768]{1,0:T(8,128)(2,1)} collective-permute-done((bf16[1536,768]{1,0:T(8,128)(2,1)}, bf16[1536,768]{1,0:T(8,128)(2,1)}, u32[]{:S(2)}, u32[]{:S(2)}) %collective-permute-start.8) | collective-permute-done | bytes 2359328 | tf_op jit(solution)/shard_map/ppermute | solution.py:217
  220.0 4.3 %gram_stage.17.refs_0_ = f32[768,768]{1,0:T(8,128)S(1)} custom-call(bf16[1536,768]{1,0:T(8,128)(2,1)} %collective-permute-done.8.refs_0_.refs_4_, bf16[3840,768]{1,0:T(8,128)(2,1)S(1)} %bitcast.31), custom_call_target="tpu_custom_call" | custom-call | flops 1811939328 | tf_op jit(solution)/shard_map/gram_stage/pallas_call | solution.py:75
  224.3 46.3 %collective-permute-done.5.refs_1_.refs_5_ = bf16[1536,768]{1,0:T(8,128)(2,1)} collective-permute-done((bf16[1536,768]{1,0:T(8,128)(2,1)}, bf16[1536,768]{1,0:T(8,128)(2,1)}, u32[]{:S(2)}, u32[]{:S(2)}) %collective-permute-start.5) | collective-permute-done | bytes 2359328 | tf_op jit(solution)/shard_map/ppermute | solution.py:217
  270.6 4.3 %gram_stage.18.refs_0_ = f32[768,768]{1,0:T(8,128)S(1)} custom-call(f32[768,768]{1,0:T(8,128)S(1)} %gram_stage.17.refs_0_, bf16[1536,768]{1,0:T(8,128)(2,1)} %collective-permute-done.5.refs_1_.refs_5_, bf16[3840,768]{1,0:T(8,128)(2,1)S(1)} %bitcast.32), custom_call_target="tpu_custom_call" | custom-call | flops 1811939328 | tf_op jit(solution)/shard_map/gram_stage/pallas_call | solution.py:75
  274.9 13.6 %collective-permute-done.4.refs_1_.refs_6_ = bf16[336,768]{1,0:T(8,128)(2,1)S(1)} collective-permute-done((bf16[336,768]{1,0:T(8,128)(2,1)}, bf16[336,768]{1,0:T(8,128)(2,1)S(1)}, u32[]{:S(2)}, u32[]{:S(2)}) %collective-permute-start.4) | collective-permute-done | bytes 516128 | tf_op jit(solution)/shard_map/ppermute | solution.py:217
  288.5 0.8 gram_stage.19.refs_0_
  289.3 0.5 gram_stage.20.refs_0_
  289.8 0.1 collective-permute-start.14
  289.9 4.1 %collective-permute-start.13 = (bf16[192,768]{1,0:T(8,128)(2,1)}, bf16[192,768]{1,0:T(8,128)(2,1)S(1)}, u32[]{:S(2)}, u32[]{:S(2)}) collective-permute-start(bf16[192,768]{1,0:T(8,128)(2,1)} %slice_bitcast_fusion.6), channel_id=1, source_target_pairs={{0,24},{2,26},{4,28},{6,30},{24,0},{26,2},{28,4},{30,6},{1,25},{3,... | collective-permute-start | bytes 884744 | tf_op jit(solution)/shard_map/ppermute | solution.py:217
  294.1 9.1 %collective-permute-done.13.refs_1_.refs_8_ = bf16[192,768]{1,0:T(8,128)(2,1)S(1)} collective-permute-done((bf16[192,768]{1,0:T(8,128)(2,1)}, bf16[192,768]{1,0:T(8,128)(2,1)S(1)}, u32[]{:S(2)}, u32[]{:S(2)}) %collective-permute-start.13) | collective-permute-done | bytes 294944 | tf_op jit(solution)/shard_map/ppermute | solution.py:217
  303.2 0.5 gram_stage.21.refs_0_
  303.7 1.1 collective-permute-done.15.refs_2_
  304.8 11.1 %far_stage.1 = f32[23040,128]{1,0:T(8,128)} custom-call(f32[2]{0:T(128)S(1)} %pad_maximum_fusion.1.energy, f32[1,768]{1,0:T(1,128)S(1)} %reshape.17.virt_row, f32[768,768]{1,0:T(8,128)S(1)} %gram_stage.21.refs_0_, f32[768,768]{1,0:T(8,128)S(1)} %collective-permute-done.14.refs_1_, bf16[192,768]{1,0:T(8,128)(2,1)S(1)} %collective-permute-done.15.refs_2_, ...), custom_call_target="tpu_custom_call" | custom-call | flops 4529848320 | bytes 11796480 | tf_op jit(solution)/shard_map/far_stage/pallas_call | solution.py:167
  (27 shorter events, 0.1 us)
Async XLA Ops:
  0.0 9.7 %copy-start = (bf16[3840,1,768]{2,0,1:T(8,128)(2,1)S(1)}, bf16[3840,1,768]{2,0,1:T(8,128)(2,1)}, u32[]{:S(2)}) copy-start(bf16[3840,1,768]{2,0,1:T(8,128)(2,1)} %param.3) | copy-start | bytes 17694724
  3.0 140.6 %collective-permute-start.6 = (bf16[3360,768]{1,0:T(8,128)(2,1)S(1)}, bf16[3360,768]{1,0:T(8,128)(2,1)S(1)}, u32[]{:S(2)}, u32[]{:S(2)}) collective-permute-start(bf16[3360,768]{1,0:T(8,128)(2,1)S(1)} %slice_bitcast_fusion), channel_id=1, source_target_pairs={{0,8},{2,10},{4,12},{6,14},{8,16},{10,18},{12,20},{14,22},{16,24},... | collective-permute-start | bytes 15482888 | tf_op jit(solution)/shard_map/ppermute | solution.py:217
  8.4 135.2 %collective-permute-start.7 = (bf16[3360,768]{1,0:T(8,128)(2,1)S(1)}, bf16[3360,768]{1,0:T(8,128)(2,1)S(1)}, u32[]{:S(2)}, u32[]{:S(2)}) collective-permute-start(bf16[3360,768]{1,0:T(8,128)(2,1)S(1)} %slice_bitcast_fusion), channel_id=1, source_target_pairs={{8,0},{10,2},{12,4},{14,6},{16,8},{18,10},{20,12},{22,14},{24,16},... | collective-permute-start | bytes 15482888 | tf_op jit(solution)/shard_map/ppermute | solution.py:217
  9.7 132.1 %collective-permute-start.9 = (bf16[384,768]{1,0:T(8,128)(2,1)S(1)}, bf16[384,768]{1,0:T(8,128)(2,1)S(1)}, u32[]{:S(2)}, u32[]{:S(2)}) collective-permute-start(bf16[384,768]{1,0:T(8,128)(2,1)S(1)} %slice_bitcast_fusion.3), channel_id=1, source_target_pairs={{0,8},{2,10},{4,12},{6,14},{8,16},{10,18},{12,20},{14,22},{16,24},... | collective-permute-start | bytes 1769480 | tf_op jit(solution)/shard_map/ppermute | solution.py:217
  14.3 128.4 %collective-permute-start.11 = (bf16[384,768]{1,0:T(8,128)(2,1)S(1)}, bf16[384,768]{1,0:T(8,128)(2,1)S(1)}, u32[]{:S(2)}, u32[]{:S(2)}) collective-permute-start(bf16[384,768]{1,0:T(8,128)(2,1)S(1)} %slice_bitcast_fusion.3), channel_id=1, source_target_pairs={{8,0},{10,2},{12,4},{14,6},{16,8},{18,10},{20,12},{22,14},{24,16},... | collective-permute-start | bytes 1769480 | tf_op jit(solution)/shard_map/ppermute | solution.py:217
  15.6 118.7 %collective-permute-start = (bf16[96,768]{1,0:T(8,128)(2,1)S(1)}, bf16[96,768]{1,0:T(8,128)(2,1)S(1)}, u32[]{:S(2)}, u32[]{:S(2)}) collective-permute-start(bf16[96,768]{1,0:T(8,128)(2,1)S(1)} %slice_bitcast_fusion.7), channel_id=1, source_target_pairs={{0,8},{2,10},{4,12},{6,14},{8,16},{10,18},{12,20},{14,22},{16,24},... | collective-permute-start | bytes 442376 | tf_op jit(solution)/shard_map/ppermute | solution.py:217
  134.4 7.5 %collective-permute-start.1 = (bf16[96,768]{1,0:T(8,128)(2,1)S(1)}, bf16[96,768]{1,0:T(8,128)(2,1)S(1)}, u32[]{:S(2)}, u32[]{:S(2)}) collective-permute-start(bf16[96,768]{1,0:T(8,128)(2,1)S(1)} %slice_bitcast_fusion.7), channel_id=1, source_target_pairs={{8,0},{10,2},{12,4},{14,6},{16,8},{18,10},{20,12},{22,14},{24,16},... | collective-permute-start | bytes 442376 | tf_op jit(solution)/shard_map/ppermute | solution.py:217
  143.5 7.0 %copy-start.1 = (bf16[3360,768]{1,0:T(8,128)(2,1)}, bf16[3360,768]{1,0:T(8,128)(2,1)S(1)}, u32[]{:S(2)}) copy-start(bf16[3360,768]{1,0:T(8,128)(2,1)S(1)} %collective-permute-done.6.refs_1_.refs_5_) | copy-start | bytes 15482884
  143.5 8.9 %copy-start.3 = (bf16[3360,768]{1,0:T(8,128)(2,1)}, bf16[3360,768]{1,0:T(8,128)(2,1)S(1)}, u32[]{:S(2)}) copy-start(bf16[3360,768]{1,0:T(8,128)(2,1)S(1)} %collective-permute-done.7.refs_1_.refs_8_) | copy-start | bytes 15482884
  152.4 26.3 %collective-permute-start.10 = (f32[768,768]{1,0:T(8,128)}, f32[768,768]{1,0:T(8,128)}, u32[]{:S(2)}, u32[]{:S(2)}) collective-permute-start(f32[768,768]{1,0:T(8,128)} %gram_stage.13.refs_0_), channel_id=1, source_target_pairs={{0,1},{1,0},{2,3},{3,2},{4,5},{5,4},{6,7},{7,6},{8,9},{9,8},{10,11... | collective-permute-start | bytes 7077896 | tf_op jit(solution)/shard_map/ppermute | solution.py:26
  159.4 10.2 %copy-start.5 = (f32[16]{0:T(128)S(1)}, f32[16]{0:T(128)}, u32[]{:S(2)}) copy-start(f32[16]{0:T(128)} %param.4) | copy-start | bytes 196
  159.4 13.2 %copy-start.6 = (f32[768]{0:T(1024)S(1)}, f32[768]{0:T(1024)}, u32[]{:S(2)}) copy-start(f32[768]{0:T(1024)} %param.5) | copy-start | bytes 9220
  159.5 60.6 %slice-start = ((s8[5898240]{0:T(1024)(128)(4,1)}), s8[1703936]{0:T(1024)(128)(4,1)S(1)}, s32[]{:S(2)}) async-start(s8[5898240]{0:T(1024)(128)(4,1)} %bitcast.29), calls=%async_computation | async-start | bytes 3407872
  161.4 21.3 %collective-permute-start.12 = (f32[768,768]{1,0:T(8,128)}, f32[768,768]{1,0:T(8,128)}, u32[]{:S(2)}, u32[]{:S(2)}) collective-permute-start(f32[768,768]{1,0:T(8,128)} %gram_stage.16.refs_2_), channel_id=1, source_target_pairs={{0,1},{1,0},{2,3},{3,2},{4,5},{5,4},{6,7},{7,6},{8,9},{9,8},{10,11... | collective-permute-start | bytes 7077896 | tf_op jit(solution)/shard_map/ppermute | solution.py:26
  161.9 58.1 %collective-permute-start.8 = (bf16[1536,768]{1,0:T(8,128)(2,1)}, bf16[1536,768]{1,0:T(8,128)(2,1)}, u32[]{:S(2)}, u32[]{:S(2)}) collective-permute-start(bf16[1536,768]{1,0:T(8,128)(2,1)} %get-tuple-element.38), channel_id=1, source_target_pairs={{0,24},{2,26},{4,28},{6,30},{24,0},{26,2},{28,4},{30,6},{1,25},{3,... | collective-permute-start | bytes 7077896 | tf_op jit(solution)/shard_map/ppermute | solution.py:217
  165.8 104.8 %collective-permute-start.5 = (bf16[1536,768]{1,0:T(8,128)(2,1)}, bf16[1536,768]{1,0:T(8,128)(2,1)}, u32[]{:S(2)}, u32[]{:S(2)}) collective-permute-start(bf16[1536,768]{1,0:T(8,128)(2,1)} %get-tuple-element.37), channel_id=1, source_target_pairs={{0,24},{2,26},{4,28},{6,30},{24,0},{26,2},{28,4},{30,6},{1,25},{3,... | collective-permute-start | bytes 7077896 | tf_op jit(solution)/shard_map/ppermute | solution.py:217
  169.5 5.0 %collective-permute-start.2 = (bf16[192,768]{1,0:T(8,128)(2,1)}, bf16[192,768]{1,0:T(8,128)(2,1)S(1)}, u32[]{:S(2)}, u32[]{:S(2)}) collective-permute-start(bf16[192,768]{1,0:T(8,128)(2,1)} %slice_bitcast_fusion.6), channel_id=1, source_target_pairs={{0,1},{1,0},{2,3},{3,2},{4,5},{5,4},{6,7},{7,6},{8,9},{9,8},{10,11... | collective-permute-start | bytes 884744 | tf_op jit(solution)/shard_map/ppermute | solution.py:26
  174.6 45.5 %slice-start.1 = ((s8[5898240]{0:T(1024)(128)(4,1)}), s8[4194304]{0:T(1024)(128)(4,1)S(1)}, s32[]{:S(2)}) async-start(s8[5898240]{0:T(1024)(128)(4,1)} %bitcast.29), calls=%async_computation.1 | async-start | bytes 8388608
  174.6 114.7 %collective-permute-start.3 = (bf16[240,768]{1,0:T(8,128)(2,1)}, bf16[240,768]{1,0:T(8,128)(2,1)S(1)}, u32[]{:S(2)}, u32[]{:S(2)}) collective-permute-start(bf16[240,768]{1,0:T(8,128)(2,1)} %slice_bitcast_fusion.5), channel_id=1, source_target_pairs={{0,24},{2,26},{4,28},{6,30},{24,0},{26,2},{28,4},{30,6},{1,25},{3,... | collective-permute-start | bytes 1105928 | tf_op jit(solution)/shard_map/ppermute | solution.py:217
  178.8 109.7 %collective-permute-start.4 = (bf16[336,768]{1,0:T(8,128)(2,1)}, bf16[336,768]{1,0:T(8,128)(2,1)S(1)}, u32[]{:S(2)}, u32[]{:S(2)}) collective-permute-start(bf16[336,768]{1,0:T(8,128)(2,1)} %slice_bitcast_fusion.4), channel_id=1, source_target_pairs={{0,24},{2,26},{4,28},{6,30},{24,0},{26,2},{28,4},{30,6},{1,25},{3,... | collective-permute-start | bytes 1548296 | tf_op jit(solution)/shard_map/ppermute | solution.py:217
  182.7 2.5 copy-start.2
  185.1 2.5 copy-start.4
  289.8 15.0 %collective-permute-start.14 = (f32[768,768]{1,0:T(8,128)S(1)}, f32[768,768]{1,0:T(8,128)S(1)}, u32[]{:S(2)}, u32[]{:S(2)}) collective-permute-start(f32[768,768]{1,0:T(8,128)S(1)} %gram_stage.20.refs_0_), channel_id=1, source_target_pairs={{0,1},{1,0},{2,3},{3,2},{4,5},{5,4},{6,7},{7,6},{8,9},{9,8},{10,11... | collective-permute-start | bytes 7077896 | tf_op jit(solution)/shard_map/ppermute | solution.py:26
  289.9 13.3 %collective-permute-start.13 = (bf16[192,768]{1,0:T(8,128)(2,1)}, bf16[192,768]{1,0:T(8,128)(2,1)S(1)}, u32[]{:S(2)}, u32[]{:S(2)}) collective-permute-start(bf16[192,768]{1,0:T(8,128)(2,1)} %slice_bitcast_fusion.6), channel_id=1, source_target_pairs={{0,24},{2,26},{4,28},{6,30},{24,0},{26,2},{28,4},{30,6},{1,25},{3,... | collective-permute-start | bytes 884744 | tf_op jit(solution)/shard_map/ppermute | solution.py:217
  303.2 1.6 collective-permute-start.15
